TPU v7x, 32 devices: a 4x4x1 block of a 4x4x8 slice. The times are simulated.
32 devices in a mesh: dp: 1 (over z), pp: 4 (over y), sp: 8 (over x, core).
Axes of the slice: x: 4, y: 4, z: 1, core: 2. Of those that a mesh axis runs over, the one named last changes fastest.
The devices are a block of a 4x4x8 slice.
Arguments:
- latent_in: float32 [4, 256, 16], P('dp', 'sp')
- pos_embed: bfloat16 [4, 256, 1152], P(None, 'sp')
- condition: bfloat16 [2, 1152], P('dp')
- step_size: float32 [2], P('dp')
- w_in: bfloat16 [16, 1152], replicated
- w_ada: bfloat16 [4, 1152, 6912], replicated
- w_qkv: bfloat16 [4, 1152, 3456], replicated
- w_o: bfloat16 [4, 1152, 1152], replicated
- w_up: bfloat16 [4, 1152, 4608], replicated
- w_down: bfloat16 [4, 4608, 1152], replicated
- b_layer: bfloat16 [4, 17280], replicated
- w_fa: bfloat16 [1152, 2304], replicated
- b_fa: bfloat16 [2304], replicated
- w_out: bfloat16 [1152, 16], replicated
- k_old: bfloat16 [4, 1024, 16, 72], P('dp')
- v_old: bfloat16 [4, 1024, 16, 72], P('dp')
Outputs:
- output: float32 [4, 256, 16], P('dp', 'sp')
All inputs are finite; a program needn't handle non-finite values.
Results may differ from a plain program's by a relative error of at most 0.0118966.
Values are sent between devices in bfloat16 or wider.
A program may use at most 768 MiB of HBM per device.

v0:
```python
import jax
import jax.numpy as jnp
from jax import lax
from jax.sharding import PartitionSpec as P

LN_EPS = 1e-6


def layer_norm(hidden):
    mean_val = jnp.mean(hidden, axis=-1, keepdims=True)
    centered = hidden - mean_val
    var_val = jnp.mean(centered * centered, axis=-1, keepdims=True)
    return centered * lax.rsqrt(var_val + LN_EPS)


def solution(mesh):
    num_stages = mesh.shape["pp"]
    split_count = mesh.shape["sp"]
    forward_perm = [(src_stage, src_stage + 1) for src_stage in range(num_stages - 1)]
    return_perm = [(num_stages - 1, 0)]
    row_spec = P("dp", "sp", None)
    full_spec = P()
    buf_spec = P("dp", None, None, None)
    in_specs = (row_spec, P(None, "sp", None), P("dp", None), P("dp"), full_spec, full_spec, full_spec, full_spec, full_spec, full_spec, full_spec, full_spec, full_spec, full_spec, buf_spec, buf_spec)

    def device_fn(latent_in, pos_embed, condition, step_size, w_in, w_ada, w_qkv, w_o, w_up, w_down, b_layer, w_fa, b_fa, w_out, k_old, v_old):
        num_patches = latent_in.shape[0]
        sub_rows = latent_in.shape[1]
        patch_rows = sub_rows * split_count
        model_width = w_in.shape[1]
        stage_layers = w_qkv.shape[0] // num_stages
        num_heads = k_old.shape[2]
        head_dim = k_old.shape[3]
        attn_scale = head_dim ** -0.5
        stage_idx = lax.axis_index("pp")
        is_last = stage_idx == num_stages - 1
        first_layer = stage_idx * stage_layers
        ada_stage = lax.dynamic_slice_in_dim(w_ada, first_layer, stage_layers, axis=0)
        qkv_stage = lax.dynamic_slice_in_dim(w_qkv, first_layer, stage_layers, axis=0)
        out_stage = lax.dynamic_slice_in_dim(w_o, first_layer, stage_layers, axis=0)
        up_stage = lax.dynamic_slice_in_dim(w_up, first_layer, stage_layers, axis=0)
        down_stage = lax.dynamic_slice_in_dim(w_down, first_layer, stage_layers, axis=0)
        bias_stage = lax.dynamic_slice_in_dim(b_layer, first_layer, stage_layers, axis=0).astype(jnp.float32)
        b_fa32 = b_fa.astype(jnp.float32)
        key_bufs = [lax.dynamic_index_in_dim(k_old, first_layer + layer_j, axis=0, keepdims=False) for layer_j in range(stage_layers)]
        value_bufs = [lax.dynamic_index_in_dim(v_old, first_layer + layer_j, axis=0, keepdims=False) for layer_j in range(stage_layers)]

        def run_layer(hidden, mod_vec, layer_j, key_buf, value_buf, row_start, is_valid):
            bias_row = bias_stage[layer_j]
            scale_attn, shift_attn, gate_attn, scale_mlp, shift_mlp, gate_mlp = jnp.split(mod_vec, 6)
            normed = (layer_norm(hidden.astype(jnp.float32)) * (1.0 + scale_attn) + shift_attn).astype(jnp.bfloat16)
            qkv_rows = (jnp.dot(normed, qkv_stage[layer_j], preferred_element_type=jnp.float32) + bias_row[6 * model_width:9 * model_width]).astype(jnp.bfloat16)
            kv_patch = lax.all_gather(qkv_rows[:, model_width:], "sp", axis=0, tiled=True)
            key_new = kv_patch[:, :model_width].reshape(patch_rows, num_heads, head_dim)
            value_new = kv_patch[:, model_width:].reshape(patch_rows, num_heads, head_dim)
            key_prev = lax.dynamic_slice_in_dim(key_buf, row_start, patch_rows, axis=0)
            value_prev = lax.dynamic_slice_in_dim(value_buf, row_start, patch_rows, axis=0)
            key_buf = lax.dynamic_update_slice_in_dim(key_buf, jnp.where(is_valid, key_new, key_prev), row_start, axis=0)
            value_buf = lax.dynamic_update_slice_in_dim(value_buf, jnp.where(is_valid, value_new, value_prev), row_start, axis=0)
            query_rows = qkv_rows[:, :model_width].reshape(sub_rows, num_heads, head_dim)
            logits = jnp.einsum("rhd,nhd->hrn", query_rows, key_buf, preferred_element_type=jnp.float32) * attn_scale
            attn_prob = jax.nn.softmax(logits, axis=-1).astype(jnp.bfloat16)
            attn_rows = jnp.einsum("hrn,nhd->rhd", attn_prob, value_buf, preferred_element_type=jnp.float32).astype(jnp.bfloat16).reshape(sub_rows, model_width)
            residual = hidden.astype(jnp.float32) + gate_attn * (jnp.dot(attn_rows, out_stage[layer_j], preferred_element_type=jnp.float32) + bias_row[9 * model_width:10 * model_width])
            mlp_in = (layer_norm(residual) * (1.0 + scale_mlp) + shift_mlp).astype(jnp.bfloat16)
            mlp_mid = jax.nn.gelu(jnp.dot(mlp_in, up_stage[layer_j], preferred_element_type=jnp.float32) + bias_row[10 * model_width:14 * model_width], approximate=True).astype(jnp.bfloat16)
            hidden = (residual + gate_mlp * (jnp.dot(mlp_mid, down_stage[layer_j], preferred_element_type=jnp.float32) + bias_row[14 * model_width:])).astype(jnp.bfloat16)
            return hidden, key_buf, value_buf

        def run_step(step_idx, x_source, latent_cur, keys_start, values_start):
            cond_act = jax.nn.silu(condition[step_idx].astype(jnp.float32)).astype(jnp.bfloat16)
            mod_stage = jnp.einsum("c,lcf->lf", cond_act, ada_stage, preferred_element_type=jnp.float32) + bias_stage[:, :6 * model_width]
            final_mod = jnp.dot(cond_act[None, :], w_fa, preferred_element_type=jnp.float32)[0] + b_fa32
            scale_out, shift_out = jnp.split(final_mod, 2)
            step_val = step_size[step_idx]

            def tick_body(tick_idx, loop_state):
                received, latent_acc, keys_in, values_in = loop_state
                patch_idx = tick_idx - stage_idx
                is_valid = (patch_idx >= 0) & (patch_idx < num_patches)
                patch_safe = jnp.clip(patch_idx, 0, num_patches - 1)
                row_start = patch_safe * patch_rows
                x_rows = lax.dynamic_index_in_dim(x_source, patch_safe, axis=0, keepdims=False)
                pos_rows = lax.dynamic_index_in_dim(pos_embed, patch_safe, axis=0, keepdims=False)
                embedded = (jnp.dot(x_rows, w_in, preferred_element_type=jnp.float32) + pos_rows.astype(jnp.float32)).astype(jnp.bfloat16)
                hidden = jnp.where(stage_idx == 0, embedded, received)
                keys_out = []
                values_out = []
                for layer_j in range(stage_layers):
                    hidden, key_buf, value_buf = run_layer(hidden, mod_stage[layer_j], layer_j, keys_in[layer_j], values_in[layer_j], row_start, is_valid)
                    keys_out.append(key_buf)
                    values_out.append(value_buf)
                out_in = (layer_norm(hidden.astype(jnp.float32)) * (1.0 + scale_out) + shift_out).astype(jnp.bfloat16)
                velocity = jnp.dot(out_in, w_out, preferred_element_type=jnp.float32)
                x_old = lax.dynamic_index_in_dim(latent_acc, patch_safe, axis=0, keepdims=False)
                x_new = jnp.where(is_valid & is_last, x_old + step_val * velocity, x_old)
                latent_acc = lax.dynamic_update_index_in_dim(latent_acc, x_new, patch_safe, axis=0)
                sent_rows = lax.ppermute(hidden, "pp", forward_perm)
                return (sent_rows, latent_acc, keys_out, values_out)

            start_state = (jnp.zeros((sub_rows, model_width), jnp.bfloat16), latent_cur, keys_start, values_start)
            end_state = lax.fori_loop(0, num_patches + num_stages - 1, tick_body, start_state)
            return end_state[1], end_state[2], end_state[3]

        latent_cur, key_bufs, value_bufs = run_step(0, latent_in.astype(jnp.bfloat16), latent_in, key_bufs, value_bufs)
        x_source = lax.ppermute(latent_cur.astype(jnp.bfloat16), "pp", return_perm)
        latent_cur, key_bufs, value_bufs = run_step(1, x_source, latent_cur, key_bufs, value_bufs)
        return lax.psum(jnp.where(is_last, latent_cur, 0.0), "pp")

    return jax.shard_map(device_fn, mesh=mesh, in_specs=in_specs, out_specs=row_spec, check_vma=False)
```

profile of v0, /device:TPU:97, one launch (start us, length us, event | category | flops | bytes accessed | tf_op | source)
XLA Modules:
  0.0 958.3 jit_solution(17117501337538272624)
XLA Ops:
  7.3 3.5 convolution_reduce_fusion
  12.4 9.9 %constant_dynamic-slice_fusion.2 = bf16[1,4608,1152]{2,1,0:T(8,128)(2,1)} fusion(bf16[4,4608,1152]{2,1,0:T(8,128)(2,1)} %param.29, s32[]{:T(128)S(6)} %select_n.178), kind=kLoop, calls=%fused_computation.237 | loop fusion | bytes 21233668 | tf_op jit(solution)/shard_map/dynamic_slice | solution.py:42
  22.3 9.9 %constant_dynamic-slice_fusion.3 = bf16[1,1152,4608]{2,1,0:T(8,128)(2,1)} fusion(bf16[4,1152,4608]{2,1,0:T(8,128)(2,1)} %param.28, s32[]{:T(128)S(6)} %select_n.178), kind=kLoop, calls=%fused_computation.238 | loop fusion | bytes 21233668 | tf_op jit(solution)/shard_map/dynamic_slice | solution.py:41
  32.2 6.9 constant_dynamic-slice_fusion.5
  39.1 3.5 constant_dynamic-slice_fusion.4
  43.3 7.7 fusion.222
  51.0 4.4 dynamic-slice_bitcast_fusion
  55.4 437.4 %while.40 = (s32[]{:T(128)}, bf16[32,1152]{1,0:T(8,128)(2,1)S(1)}, f32[4,32,16]{1,2,0:T(8,128)S(1)}, bf16[1024,16,72]{0,2,1:T(8,128)(2,1)S(1)}, bf16[1024,16,72]...) while((s32[]{:T(128)}, bf16[32,1152]{1,0:T(8,128)(2,1)S(1)}, ...), condition=%wide.region_9.10_spmd, body=%wide.region_0.9_spmd.sunk | while | flops 1180118528 | bytes 66999408 | solution.py:102
  57.2 4.6 fusion.314
  62.9 24.8 %all-gather.3.cloned.1.call-done = bf16[256,2304]{1,0:T(8,128)(2,1)} async-done(((bf16[32,2304]{1,0:T(8,128)(2,1)}), bf16[256,2304]{1,0:T(8,128)(2,1)}) %all-gather.3.cloned.1.call-update) | async-done | bytes 1179664 | tf_op jit(solution)/shard_map/while/body/eval_jaxpr/all_gather | solution.py:53
  104.8 10.9 %convert_reduce_fusion.4 = (f32[32]{0:T(128)S(1)}, bf16[32,1152]{1,0:T(8,128)(2,1)S(1)}) fusion(f32[32,1152]{1,0:T(8,128)S(1)} %get-tuple-element.1228, f32[1152]{0:T(1024)S(1)} %get-tuple-element.1229, bf16[1,4608,1152]{2,1,0:T(8,128)(2,1)} %get-tuple-element.1344, bf16[1,1152,4608]{2,1,0:T(8,128)(2,1)} %get-tuple-element.1343, ...), kind=kOutput, calls=%fused_computation.52.clone.1 | convolution fusion | flops 681357312 | bytes 21492096 | tf_op jit(solution)/shard_map/while/body/eval_jaxpr/dot_general | solution.py:67
  121.7 4.6 fusion.314
  127.4 22.3 %all-gather.3.cloned.1.call-done = bf16[256,2304]{1,0:T(8,128)(2,1)} async-done(((bf16[32,2304]{1,0:T(8,128)(2,1)}), bf16[256,2304]{1,0:T(8,128)(2,1)}) %all-gather.3.cloned.1.call-update) | async-done | bytes 1179664 | tf_op jit(solution)/shard_map/while/body/eval_jaxpr/all_gather | solution.py:53
  160.6 3.3 fusion.318
  166.8 10.9 %convert_reduce_fusion.4 = (f32[32]{0:T(128)S(1)}, bf16[32,1152]{1,0:T(8,128)(2,1)S(1)}) fusion(f32[32,1152]{1,0:T(8,128)S(1)} %get-tuple-element.1228, f32[1152]{0:T(1024)S(1)} %get-tuple-element.1229, bf16[1,4608,1152]{2,1,0:T(8,128)(2,1)} %get-tuple-element.1344, bf16[1,1152,4608]{2,1,0:T(8,128)(2,1)} %get-tuple-element.1343, ...), kind=kOutput, calls=%fused_computation.52.clone.1 | convolution fusion | flops 681357312 | bytes 21492096 | tf_op jit(solution)/shard_map/while/body/eval_jaxpr/dot_general | solution.py:67
  183.8 4.6 fusion.314
  189.6 22.1 %all-gather.3.cloned.1.call-done = bf16[256,2304]{1,0:T(8,128)(2,1)} async-done(((bf16[32,2304]{1,0:T(8,128)(2,1)}), bf16[256,2304]{1,0:T(8,128)(2,1)}) %all-gather.3.cloned.1.call-update) | async-done | bytes 1179664 | tf_op jit(solution)/shard_map/while/body/eval_jaxpr/all_gather | solution.py:53
  222.6 3.3 fusion.318
  228.8 10.9 %convert_reduce_fusion.4 = (f32[32]{0:T(128)S(1)}, bf16[32,1152]{1,0:T(8,128)(2,1)S(1)}) fusion(f32[32,1152]{1,0:T(8,128)S(1)} %get-tuple-element.1228, f32[1152]{0:T(1024)S(1)} %get-tuple-element.1229, bf16[1,4608,1152]{2,1,0:T(8,128)(2,1)} %get-tuple-element.1344, bf16[1,1152,4608]{2,1,0:T(8,128)(2,1)} %get-tuple-element.1343, ...), kind=kOutput, calls=%fused_computation.52.clone.1 | convolution fusion | flops 681357312 | bytes 21492096 | tf_op jit(solution)/shard_map/while/body/eval_jaxpr/dot_general | solution.py:67
  245.8 4.6 fusion.314
  251.5 22.3 %all-gather.3.cloned.1.call-done = bf16[256,2304]{1,0:T(8,128)(2,1)} async-done(((bf16[32,2304]{1,0:T(8,128)(2,1)}), bf16[256,2304]{1,0:T(8,128)(2,1)}) %all-gather.3.cloned.1.call-update) | async-done | bytes 1179664 | tf_op jit(solution)/shard_map/while/body/eval_jaxpr/all_gather | solution.py:53
  284.7 3.3 fusion.318
  290.9 10.9 %convert_reduce_fusion.4 = (f32[32]{0:T(128)S(1)}, bf16[32,1152]{1,0:T(8,128)(2,1)S(1)}) fusion(f32[32,1152]{1,0:T(8,128)S(1)} %get-tuple-element.1228, f32[1152]{0:T(1024)S(1)} %get-tuple-element.1229, bf16[1,4608,1152]{2,1,0:T(8,128)(2,1)} %get-tuple-element.1344, bf16[1,1152,4608]{2,1,0:T(8,128)(2,1)} %get-tuple-element.1343, ...), kind=kOutput, calls=%fused_computation.52.clone.1 | convolution fusion | flops 681357312 | bytes 21492096 | tf_op jit(solution)/shard_map/while/body/eval_jaxpr/dot_general | solution.py:67
  308.0 4.6 fusion.314
  313.7 22.3 %all-gather.3.cloned.1.call-done = bf16[256,2304]{1,0:T(8,128)(2,1)} async-done(((bf16[32,2304]{1,0:T(8,128)(2,1)}), bf16[256,2304]{1,0:T(8,128)(2,1)}) %all-gather.3.cloned.1.call-update) | async-done | bytes 1179664 | tf_op jit(solution)/shard_map/while/body/eval_jaxpr/all_gather | solution.py:53
  352.9 10.9 %convert_reduce_fusion.4 = (f32[32]{0:T(128)S(1)}, bf16[32,1152]{1,0:T(8,128)(2,1)S(1)}) fusion(f32[32,1152]{1,0:T(8,128)S(1)} %get-tuple-element.1228, f32[1152]{0:T(1024)S(1)} %get-tuple-element.1229, bf16[1,4608,1152]{2,1,0:T(8,128)(2,1)} %get-tuple-element.1344, bf16[1,1152,4608]{2,1,0:T(8,128)(2,1)} %get-tuple-element.1343, ...), kind=kOutput, calls=%fused_computation.52.clone.1 | convolution fusion | flops 681357312 | bytes 21492096 | tf_op jit(solution)/shard_map/while/body/eval_jaxpr/dot_general | solution.py:67
  363.8 3.3 collective-permute-start
  370.1 4.6 fusion.314
  375.9 22.3 %all-gather.3.cloned.1.call-done = bf16[256,2304]{1,0:T(8,128)(2,1)} async-done(((bf16[32,2304]{1,0:T(8,128)(2,1)}), bf16[256,2304]{1,0:T(8,128)(2,1)}) %all-gather.3.cloned.1.call-update) | async-done | bytes 1179664 | tf_op jit(solution)/shard_map/while/body/eval_jaxpr/all_gather | solution.py:53
  408.9 3.3 fusion.318
  415.1 10.9 %convert_reduce_fusion.4 = (f32[32]{0:T(128)S(1)}, bf16[32,1152]{1,0:T(8,128)(2,1)S(1)}) fusion(f32[32,1152]{1,0:T(8,128)S(1)} %get-tuple-element.1228, f32[1152]{0:T(1024)S(1)} %get-tuple-element.1229, bf16[1,4608,1152]{2,1,0:T(8,128)(2,1)} %get-tuple-element.1344, bf16[1,1152,4608]{2,1,0:T(8,128)(2,1)} %get-tuple-element.1343, ...), kind=kOutput, calls=%fused_computation.52.clone.1 | convolution fusion | flops 681357312 | bytes 21492096 | tf_op jit(solution)/shard_map/while/body/eval_jaxpr/dot_general | solution.py:67
  432.1 4.6 fusion.314
  437.9 22.5 %all-gather.3.cloned.1.call-done = bf16[256,2304]{1,0:T(8,128)(2,1)} async-done(((bf16[32,2304]{1,0:T(8,128)(2,1)}), bf16[256,2304]{1,0:T(8,128)(2,1)}) %all-gather.3.cloned.1.call-update) | async-done | bytes 1179664 | tf_op jit(solution)/shard_map/while/body/eval_jaxpr/all_gather | solution.py:53
  477.3 10.9 %convert_reduce_fusion.4 = (f32[32]{0:T(128)S(1)}, bf16[32,1152]{1,0:T(8,128)(2,1)S(1)}) fusion(f32[32,1152]{1,0:T(8,128)S(1)} %get-tuple-element.1228, f32[1152]{0:T(1024)S(1)} %get-tuple-element.1229, bf16[1,4608,1152]{2,1,0:T(8,128)(2,1)} %get-tuple-element.1344, bf16[1,1152,4608]{2,1,0:T(8,128)(2,1)} %get-tuple-element.1343, ...), kind=kOutput, calls=%fused_computation.52.clone.1 | convolution fusion | flops 681357312 | bytes 21492096 | tf_op jit(solution)/shard_map/while/body/eval_jaxpr/dot_general | solution.py:67
  494.1 7.7 fusion.225
  501.8 434.9 %while.41 = (s32[]{:T(128)}, bf16[32,1152]{1,0:T(8,128)(2,1)S(1)}, f32[4,32,16]{1,2,0:T(8,128)S(1)}, bf16[1024,16,72]{0,2,1:T(8,128)(2,1)S(1)}, bf16[1024,16,72]...) while((s32[]{:T(128)}, bf16[32,1152]{1,0:T(8,128)(2,1)S(1)}, ...), condition=%wide.region_19.20_spmd, body=%wide.region_10.19_spmd.sunk | while | flops 1180118528 | bytes 66999408 | solution.py:102
  503.7 4.6 fusion.333
  509.4 22.2 %all-gather.5.cloned.1.call-done = bf16[256,2304]{1,0:T(8,128)(2,1)} async-done(((bf16[32,2304]{1,0:T(8,128)(2,1)}), bf16[256,2304]{1,0:T(8,128)(2,1)}) %all-gather.5.cloned.1.call-update) | async-done | bytes 1179664 | tf_op jit(solution)/shard_map/while/body/eval_jaxpr/all_gather | solution.py:53
  542.5 3.3 fusion.337
  548.7 10.9 %convert_reduce_fusion.5 = (f32[32]{0:T(128)S(1)}, bf16[32,1152]{1,0:T(8,128)(2,1)S(1)}) fusion(f32[32,1152]{1,0:T(8,128)S(1)} %get-tuple-element.1267, f32[1152]{0:T(1024)S(1)} %get-tuple-element.1268, bf16[1,4608,1152]{2,1,0:T(8,128)(2,1)} %get-tuple-element.1425, bf16[1,1152,4608]{2,1,0:T(8,128)(2,1)} %get-tuple-element.1424, ...), kind=kOutput, calls=%fused_computation.157.clone.1 | convolution fusion | flops 681357312 | bytes 21492096 | tf_op jit(solution)/shard_map/while/body/eval_jaxpr/dot_general | solution.py:67
  565.6 4.6 fusion.333
  571.3 22.3 %all-gather.5.cloned.1.call-done = bf16[256,2304]{1,0:T(8,128)(2,1)} async-done(((bf16[32,2304]{1,0:T(8,128)(2,1)}), bf16[256,2304]{1,0:T(8,128)(2,1)}) %all-gather.5.cloned.1.call-update) | async-done | bytes 1179664 | tf_op jit(solution)/shard_map/while/body/eval_jaxpr/all_gather | solution.py:53
  604.5 3.3 fusion.337
  610.7 10.9 %convert_reduce_fusion.5 = (f32[32]{0:T(128)S(1)}, bf16[32,1152]{1,0:T(8,128)(2,1)S(1)}) fusion(f32[32,1152]{1,0:T(8,128)S(1)} %get-tuple-element.1267, f32[1152]{0:T(1024)S(1)} %get-tuple-element.1268, bf16[1,4608,1152]{2,1,0:T(8,128)(2,1)} %get-tuple-element.1425, bf16[1,1152,4608]{2,1,0:T(8,128)(2,1)} %get-tuple-element.1424, ...), kind=kOutput, calls=%fused_computation.157.clone.1 | convolution fusion | flops 681357312 | bytes 21492096 | tf_op jit(solution)/shard_map/while/body/eval_jaxpr/dot_general | solution.py:67
  627.7 4.6 fusion.333
  633.5 22.1 %all-gather.5.cloned.1.call-done = bf16[256,2304]{1,0:T(8,128)(2,1)} async-done(((bf16[32,2304]{1,0:T(8,128)(2,1)}), bf16[256,2304]{1,0:T(8,128)(2,1)}) %all-gather.5.cloned.1.call-update) | async-done | bytes 1179664 | tf_op jit(solution)/shard_map/while/body/eval_jaxpr/all_gather | solution.py:53
  666.5 3.3 fusion.337
  672.7 10.9 %convert_reduce_fusion.5 = (f32[32]{0:T(128)S(1)}, bf16[32,1152]{1,0:T(8,128)(2,1)S(1)}) fusion(f32[32,1152]{1,0:T(8,128)S(1)} %get-tuple-element.1267, f32[1152]{0:T(1024)S(1)} %get-tuple-element.1268, bf16[1,4608,1152]{2,1,0:T(8,128)(2,1)} %get-tuple-element.1425, bf16[1,1152,4608]{2,1,0:T(8,128)(2,1)} %get-tuple-element.1424, ...), kind=kOutput, calls=%fused_computation.157.clone.1 | convolution fusion | flops 681357312 | bytes 21492096 | tf_op jit(solution)/shard_map/while/body/eval_jaxpr/dot_general | solution.py:67
  689.7 4.6 fusion.333
  695.5 22.3 %all-gather.5.cloned.1.call-done = bf16[256,2304]{1,0:T(8,128)(2,1)} async-done(((bf16[32,2304]{1,0:T(8,128)(2,1)}), bf16[256,2304]{1,0:T(8,128)(2,1)}) %all-gather.5.cloned.1.call-update) | async-done | bytes 1179664 | tf_op jit(solution)/shard_map/while/body/eval_jaxpr/all_gather | solution.py:53
  734.8 10.9 %convert_reduce_fusion.5 = (f32[32]{0:T(128)S(1)}, bf16[32,1152]{1,0:T(8,128)(2,1)S(1)}) fusion(f32[32,1152]{1,0:T(8,128)S(1)} %get-tuple-element.1267, f32[1152]{0:T(1024)S(1)} %get-tuple-element.1268, bf16[1,4608,1152]{2,1,0:T(8,128)(2,1)} %get-tuple-element.1425, bf16[1,1152,4608]{2,1,0:T(8,128)(2,1)} %get-tuple-element.1424, ...), kind=kOutput, calls=%fused_computation.157.clone.1 | convolution fusion | flops 681357312 | bytes 21492096 | tf_op jit(solution)/shard_map/while/body/eval_jaxpr/dot_general | solution.py:67
  751.9 4.6 fusion.333
  757.6 22.3 %all-gather.5.cloned.1.call-done = bf16[256,2304]{1,0:T(8,128)(2,1)} async-done(((bf16[32,2304]{1,0:T(8,128)(2,1)}), bf16[256,2304]{1,0:T(8,128)(2,1)}) %all-gather.5.cloned.1.call-update) | async-done | bytes 1179664 | tf_op jit(solution)/shard_map/while/body/eval_jaxpr/all_gather | solution.py:53
  790.6 3.3 fusion.337
  796.8 10.9 %convert_reduce_fusion.5 = (f32[32]{0:T(128)S(1)}, bf16[32,1152]{1,0:T(8,128)(2,1)S(1)}) fusion(f32[32,1152]{1,0:T(8,128)S(1)} %get-tuple-element.1267, f32[1152]{0:T(1024)S(1)} %get-tuple-element.1268, bf16[1,4608,1152]{2,1,0:T(8,128)(2,1)} %get-tuple-element.1425, bf16[1,1152,4608]{2,1,0:T(8,128)(2,1)} %get-tuple-element.1424, ...), kind=kOutput, calls=%fused_computation.157.clone.1 | convolution fusion | flops 681357312 | bytes 21492096 | tf_op jit(solution)/shard_map/while/body/eval_jaxpr/dot_general | solution.py:67
  807.8 3.3 collective-permute-start.1
  814.0 4.6 fusion.333
  819.8 22.3 %all-gather.5.cloned.1.call-done = bf16[256,2304]{1,0:T(8,128)(2,1)} async-done(((bf16[32,2304]{1,0:T(8,128)(2,1)}), bf16[256,2304]{1,0:T(8,128)(2,1)}) %all-gather.5.cloned.1.call-update) | async-done | bytes 1179664 | tf_op jit(solution)/shard_map/while/body/eval_jaxpr/all_gather | solution.py:53
  859.0 10.9 %convert_reduce_fusion.5 = (f32[32]{0:T(128)S(1)}, bf16[32,1152]{1,0:T(8,128)(2,1)S(1)}) fusion(f32[32,1152]{1,0:T(8,128)S(1)} %get-tuple-element.1267, f32[1152]{0:T(1024)S(1)} %get-tuple-element.1268, bf16[1,4608,1152]{2,1,0:T(8,128)(2,1)} %get-tuple-element.1425, bf16[1,1152,4608]{2,1,0:T(8,128)(2,1)} %get-tuple-element.1424, ...), kind=kOutput, calls=%fused_computation.157.clone.1 | convolution fusion | flops 681357312 | bytes 21492096 | tf_op jit(solution)/shard_map/while/body/eval_jaxpr/dot_general | solution.py:67
  876.1 4.6 fusion.333
  881.8 22.5 %all-gather.5.cloned.1.call-done = bf16[256,2304]{1,0:T(8,128)(2,1)} async-done(((bf16[32,2304]{1,0:T(8,128)(2,1)}), bf16[256,2304]{1,0:T(8,128)(2,1)}) %all-gather.5.cloned.1.call-update) | async-done | bytes 1179664 | tf_op jit(solution)/shard_map/while/body/eval_jaxpr/all_gather | solution.py:53
  915.0 3.3 fusion.337
  921.2 10.9 %convert_reduce_fusion.5 = (f32[32]{0:T(128)S(1)}, bf16[32,1152]{1,0:T(8,128)(2,1)S(1)}) fusion(f32[32,1152]{1,0:T(8,128)S(1)} %get-tuple-element.1267, f32[1152]{0:T(1024)S(1)} %get-tuple-element.1268, bf16[1,4608,1152]{2,1,0:T(8,128)(2,1)} %get-tuple-element.1425, bf16[1,1152,4608]{2,1,0:T(8,128)(2,1)} %get-tuple-element.1424, ...), kind=kOutput, calls=%fused_computation.157.clone.1 | convolution fusion | flops 681357312 | bytes 21492096 | tf_op jit(solution)/shard_map/while/body/eval_jaxpr/dot_general | solution.py:67
  936.7 15.0 %psum.7 = f32[4,32,16]{1,2,0:T(8,128)} all-reduce(f32[4,32,16]{1,2,0:T(8,128)S(1)} %broadcast_select_fusion), channel_id=1, replica_groups=mesh['dp'=1,'pp'=4,'sp'=8] {'pp'}, use_global_device_ids=true, to_apply=%region_20.21 | all-reduce | flops 2048 | bytes 16384 | tf_op jit(solution)/shard_map/psum | solution.py:108
  (547 shorter events, 304.6 us)
Async XLA Ops:
  7.3 4.1 copy-start.2
  7.3 4.1 copy-start.4
  11.4 0.9 copy-start.5
  39.1 3.5 copy-start.6
  39.1 3.6 copy-start.7
  51.0 4.4 copy-start.3
  55.6 32.2 %all-gather.3.cloned.1.call-start = ((), (), s32[]{:S(2)}) async-start(), calls=%async_computation | async-start | bytes 1327104 | tf_op jit(solution)/shard_map/while/body/eval_jaxpr/all_gather | solution.py:53
  96.6 1.3 copy-start
  104.8 14.1 %copy-start.8 = (bf16[1152,16]{0,1:T(8,128)(2,1)S(1)}, bf16[1152,16]{0,1:T(8,128)(2,1)}, u32[]{:S(2)}) copy-start(bf16[1152,16]{0,1:T(8,128)(2,1)} %get-tuple-element.1349) | copy-start | bytes 110596 | tf_op jit(solution)/shard_map/while
  115.8 4.4 collective-permute-start
  120.1 29.6 %all-gather.3.cloned.1.call-start = ((), (), s32[]{:S(2)}) async-start(), calls=%async_computation | async-start | bytes 1327104 | tf_op jit(solution)/shard_map/while/body/eval_jaxpr/all_gather | solution.py:53
  158.6 1.3 copy-start
  166.8 14.3 %copy-start.8 = (bf16[1152,16]{0,1:T(8,128)(2,1)S(1)}, bf16[1152,16]{0,1:T(8,128)(2,1)}, u32[]{:S(2)}) copy-start(bf16[1152,16]{0,1:T(8,128)(2,1)} %get-tuple-element.1349) | copy-start | bytes 110596 | tf_op jit(solution)/shard_map/while
  177.7 4.5 collective-permute-start
  182.3 29.4 %all-gather.3.cloned.1.call-start = ((), (), s32[]{:S(2)}) async-start(), calls=%async_computation | async-start | bytes 1327104 | tf_op jit(solution)/shard_map/while/body/eval_jaxpr/all_gather | solution.py:53
  220.6 1.3 copy-start
  228.8 14.3 %copy-start.8 = (bf16[1152,16]{0,1:T(8,128)(2,1)S(1)}, bf16[1152,16]{0,1:T(8,128)(2,1)}, u32[]{:S(2)}) copy-start(bf16[1152,16]{0,1:T(8,128)(2,1)} %get-tuple-element.1349) | copy-start | bytes 110596 | tf_op jit(solution)/shard_map/while
  239.7 4.5 collective-permute-start
  244.3 29.6 %all-gather.3.cloned.1.call-start = ((), (), s32[]{:S(2)}) async-start(), calls=%async_computation | async-start | bytes 1327104 | tf_op jit(solution)/shard_map/while/body/eval_jaxpr/all_gather | solution.py:53
  282.7 1.3 copy-start
  290.9 14.3 %copy-start.8 = (bf16[1152,16]{0,1:T(8,128)(2,1)S(1)}, bf16[1152,16]{0,1:T(8,128)(2,1)}, u32[]{:S(2)}) copy-start(bf16[1152,16]{0,1:T(8,128)(2,1)} %get-tuple-element.1349) | copy-start | bytes 110596 | tf_op jit(solution)/shard_map/while
  301.9 4.6 collective-permute-start
  306.4 29.5 %all-gather.3.cloned.1.call-start = ((), (), s32[]{:S(2)}) async-start(), calls=%async_computation | async-start | bytes 1327104 | tf_op jit(solution)/shard_map/while/body/eval_jaxpr/all_gather | solution.py:53
  344.7 1.3 copy-start
  352.9 14.5 %copy-start.8 = (bf16[1152,16]{0,1:T(8,128)(2,1)S(1)}, bf16[1152,16]{0,1:T(8,128)(2,1)}, u32[]{:S(2)}) copy-start(bf16[1152,16]{0,1:T(8,128)(2,1)} %get-tuple-element.1349) | copy-start | bytes 110596 | tf_op jit(solution)/shard_map/while
  363.8 4.7 collective-permute-start
  368.6 29.6 %all-gather.3.cloned.1.call-start = ((), (), s32[]{:S(2)}) async-start(), calls=%async_computation | async-start | bytes 1327104 | tf_op jit(solution)/shard_map/while/body/eval_jaxpr/all_gather | solution.py:53
  406.9 1.3 copy-start
  415.1 14.3 %copy-start.8 = (bf16[1152,16]{0,1:T(8,128)(2,1)S(1)}, bf16[1152,16]{0,1:T(8,128)(2,1)}, u32[]{:S(2)}) copy-start(bf16[1152,16]{0,1:T(8,128)(2,1)} %get-tuple-element.1349) | copy-start | bytes 110596 | tf_op jit(solution)/shard_map/while
  426.1 4.5 collective-permute-start
  430.6 29.8 %all-gather.3.cloned.1.call-start = ((), (), s32[]{:S(2)}) async-start(), calls=%async_computation | async-start | bytes 1327104 | tf_op jit(solution)/shard_map/while/body/eval_jaxpr/all_gather | solution.py:53
  469.1 1.3 copy-start
  477.3 14.3 %copy-start.8 = (bf16[1152,16]{0,1:T(8,128)(2,1)S(1)}, bf16[1152,16]{0,1:T(8,128)(2,1)}, u32[]{:S(2)}) copy-start(bf16[1152,16]{0,1:T(8,128)(2,1)} %get-tuple-element.1349) | copy-start | bytes 110596 | tf_op jit(solution)/shard_map/while
  488.2 4.5 collective-permute-start
  492.8 9.0 collective-permute-start.2
  502.1 29.6 %all-gather.5.cloned.1.call-start = ((), (), s32[]{:S(2)}) async-start(), calls=%async_computation.1 | async-start | bytes 1327104 | tf_op jit(solution)/shard_map/while/body/eval_jaxpr/all_gather | solution.py:53
  540.5 1.3 copy-start.1
  548.7 14.1 %copy-start.9 = (bf16[1152,16]{0,1:T(8,128)(2,1)S(1)}, bf16[1152,16]{0,1:T(8,128)(2,1)}, u32[]{:S(2)}) copy-start(bf16[1152,16]{0,1:T(8,128)(2,1)} %get-tuple-element.1430) | copy-start | bytes 110596 | tf_op jit(solution)/shard_map/while
  559.7 4.4 collective-permute-start.1
  564.0 29.6 %all-gather.5.cloned.1.call-start = ((), (), s32[]{:S(2)}) async-start(), calls=%async_computation.1 | async-start | bytes 1327104 | tf_op jit(solution)/shard_map/while/body/eval_jaxpr/all_gather | solution.py:53
  602.5 1.3 copy-start.1
  610.7 14.3 %copy-start.9 = (bf16[1152,16]{0,1:T(8,128)(2,1)S(1)}, bf16[1152,16]{0,1:T(8,128)(2,1)}, u32[]{:S(2)}) copy-start(bf16[1152,16]{0,1:T(8,128)(2,1)} %get-tuple-element.1430) | copy-start | bytes 110596 | tf_op jit(solution)/shard_map/while
  621.6 4.5 collective-permute-start.1
  626.2 29.4 %all-gather.5.cloned.1.call-start = ((), (), s32[]{:S(2)}) async-start(), calls=%async_computation.1 | async-start | bytes 1327104 | tf_op jit(solution)/shard_map/while/body/eval_jaxpr/all_gather | solution.py:53
  664.5 1.3 copy-start.1
  672.7 14.3 %copy-start.9 = (bf16[1152,16]{0,1:T(8,128)(2,1)S(1)}, bf16[1152,16]{0,1:T(8,128)(2,1)}, u32[]{:S(2)}) copy-start(bf16[1152,16]{0,1:T(8,128)(2,1)} %get-tuple-element.1430) | copy-start | bytes 110596 | tf_op jit(solution)/shard_map/while
  683.7 4.5 collective-permute-start.1
  688.2 29.6 %all-gather.5.cloned.1.call-start = ((), (), s32[]{:S(2)}) async-start(), calls=%async_computation.1 | async-start | bytes 1327104 | tf_op jit(solution)/shard_map/while/body/eval_jaxpr/all_gather | solution.py:53
  726.6 1.3 copy-start.1
  734.8 14.3 %copy-start.9 = (bf16[1152,16]{0,1:T(8,128)(2,1)S(1)}, bf16[1152,16]{0,1:T(8,128)(2,1)}, u32[]{:S(2)}) copy-start(bf16[1152,16]{0,1:T(8,128)(2,1)} %get-tuple-element.1430) | copy-start | bytes 110596 | tf_op jit(solution)/shard_map/while
  745.8 4.6 collective-permute-start.1
  750.3 29.5 %all-gather.5.cloned.1.call-start = ((), (), s32[]{:S(2)}) async-start(), calls=%async_computation.1 | async-start | bytes 1327104 | tf_op jit(solution)/shard_map/while/body/eval_jaxpr/all_gather | solution.py:53
  788.6 1.3 copy-start.1
  796.8 14.5 %copy-start.9 = (bf16[1152,16]{0,1:T(8,128)(2,1)S(1)}, bf16[1152,16]{0,1:T(8,128)(2,1)}, u32[]{:S(2)}) copy-start(bf16[1152,16]{0,1:T(8,128)(2,1)} %get-tuple-element.1430) | copy-start | bytes 110596 | tf_op jit(solution)/shard_map/while
  807.8 4.7 collective-permute-start.1
  812.5 29.6 %all-gather.5.cloned.1.call-start = ((), (), s32[]{:S(2)}) async-start(), calls=%async_computation.1 | async-start | bytes 1327104 | tf_op jit(solution)/shard_map/while/body/eval_jaxpr/all_gather | solution.py:53
  850.8 1.3 copy-start.1
  859.0 14.3 %copy-start.9 = (bf16[1152,16]{0,1:T(8,128)(2,1)S(1)}, bf16[1152,16]{0,1:T(8,128)(2,1)}, u32[]{:S(2)}) copy-start(bf16[1152,16]{0,1:T(8,128)(2,1)} %get-tuple-element.1430) | copy-start | bytes 110596 | tf_op jit(solution)/shard_map/while
  870.0 4.5 collective-permute-start.1
  874.5 29.8 %all-gather.5.cloned.1.call-start = ((), (), s32[]{:S(2)}) async-start(), calls=%async_computation.1 | async-start | bytes 1327104 | tf_op jit(solution)/shard_map/while/body/eval_jaxpr/all_gather | solution.py:53
  913.0 1.3 copy-start.1
  921.2 14.3 %copy-start.9 = (bf16[1152,16]{0,1:T(8,128)(2,1)S(1)}, bf16[1152,16]{0,1:T(8,128)(2,1)}, u32[]{:S(2)}) copy-start(bf16[1152,16]{0,1:T(8,128)(2,1)} %get-tuple-element.1430) | copy-start | bytes 110596 | tf_op jit(solution)/shard_map/while
  932.1 4.5 collective-permute-start.1
Sparse Core Ops, SparseCore 0:
  62.7 25.0 all-gather.2
  127.1 22.5 all-gather.2
  189.3 22.3 all-gather.2
  251.3 22.5 all-gather.2
  313.4 22.4 all-gather.2
  375.6 22.5 all-gather.2
  437.6 22.7 all-gather.2
  509.1 22.4 all-gather.4
  571.0 22.5 all-gather.4
  633.2 22.3 all-gather.4
  695.2 22.5 all-gather.4
  757.4 22.4 all-gather.4
  819.5 22.5 all-gather.4
  881.5 22.7 all-gather.4
where the time goes:
time: 966 us; the launch traced here: 958 us
  matrix products  353 us (37%)
  waiting for transfers between devices  321 us (33%)
  local copies, waits for them, and re-layouts  154 us (16%)
  other arithmetic  53.5 us (6%)
  starting transfers between devices  45.5 us (5%)
  blocking collectives  15 us (2%)
  between operations  13.2 us (1%)
    all_gather x14, waiting for transfers between devices, run_layer(): lax.all_gather(qkv_rows[:, model_width:], 'sp', axis=0, tiled=True)  315 us
    dot_general x14, matrix products, run_layer(): jnp.dot(mlp_mid, down_stage[layer_j], preferred_element_type=jnp.float32)  153 us
    dot_general x14, matrix products, run_layer(): jnp.dot(normed, qkv_stage[layer_j], preferred_element_type=jnp.float32)  64.5 us
    slice x28, local copies, waits for them, and re-layouts, run_layer(): key_new = kv_patch[:, :model_width].reshape(patch_rows, num_heads, head_dim)  50.7 us
    dot_general x14, matrix products, run_layer(): jnp.einsum('hrn,nhd->rhd', attn_prob, value_buf, preferred_element_type=j...  46.6 us
    ppermute x14, starting transfers between devices, tick_body(): sent_rows = lax.ppermute(hidden, 'pp', forward_perm)  44.1 us
    dynamic_update_slice x14, other arithmetic, run_layer(): lax.dynamic_update_slice_in_dim(key_buf, jnp.where(is_valid, key_new, key...  34.3 us
    dot_general x14, matrix products, run_layer(): jnp.dot(attn_rows, out_stage[layer_j], preferred_element_type=jnp.float32)  33.9 us
  transfers between devices with their start and end apart: 29, of which 28 were waited for; matrix products, arithmetic and copies ran while one was open for 3% of the time, Pallas kernels for 0%

commit v1 on v0

v1 whole, which is shorter than its diff:
```python
import functools

import jax
import jax.numpy as jnp
from jax import lax
from jax.experimental import pallas as pl
from jax.experimental.pallas import tpu as pltpu
from jax.sharding import PartitionSpec as P

LN_EPS = 1e-6
LANES = 128
LOG2_E = 1.4426950408889634
MESH = pl.DeviceIdType.MESH


def normalize(hidden):
    mean_val = jnp.mean(hidden, axis=-1, keepdims=True)
    centered = hidden - mean_val
    var_val = jnp.mean(centered * centered, axis=-1, keepdims=True)
    return centered * lax.rsqrt(var_val + LN_EPS)


def kernel(dims, latent_ref, pos_ref, cond_ref, step_ref, w_in_ref, b_layer_ref, b_fa_ref, w_out_ref,
           old_hbm, w_ada_hbm, w_fa_hbm, w_qkv_hbm, w_o_hbm, w_up_hbm, w_down_hbm,
           out_ref,
           ada_w, fa_w, qkv_w, o_w, up_w, down_w, kv, qkv_s, msg, o_msg, o_in, ada_msg, ada_in,
           mod_s, fmod_s, bias_s, hid_s, lat_s, pos_s, mid_s, lat_in, pos_in, out_in,
           w_sem, load_sem, ada_ss, ada_rs, qkv_ss, qkv_rs, o_ss, o_rs, fwd_ss, fwd_rs, in_ss, in_rs, out_ss, out_rs):
    (chips_x, chips_y, layers, patches, block_rows, width, heads, head_dim) = dims
    chips = chips_x * chips_y
    group = chips_y // 2
    patch_rows = block_rows * 2 * chips_x
    half_rows = 2 * patch_rows
    dp = lax.axis_index("dp")
    y = lax.axis_index("pp")
    s = lax.axis_index("sp")
    x = s // 2
    c = s % 2
    g = y * chips_x + x
    j_own = y // group
    patch = 2 * c + j_own
    row_own = pl.multiple_of(patch * patch_rows + (2 * x + y % 2) * block_rows, block_rows)

    def chip_dev(chip, core):
        return (dp, chip // chips_x, 2 * (chip % chips_x) + core)

    def local_row(chip):
        cy = chip // chips_x
        cx = chip % chips_x
        return (cy // group) * patch_rows + (2 * cx + cy % 2) * block_rows

    def half_row(chip):
        return pl.multiple_of(c * half_rows + local_row(chip), block_rows)

    partner = (dp, y, 2 * x + (1 - c))

    ada_tiles = ada_w.shape[1] // LANES
    ada_total = w_ada_hbm.shape[2] // LANES
    parts = chips // layers
    fa_tiles = fa_w.shape[1] // LANES
    fa_total = w_fa_hbm.shape[1] // LANES

    ada_layer = g // parts
    ada_col = pl.multiple_of(jnp.minimum(ada_tiles * (g % parts), ada_total - ada_tiles) * LANES, LANES)
    fa_col = pl.multiple_of(jnp.minimum(fa_tiles * g, fa_total - fa_tiles) * LANES, LANES)
    ada_copy = pltpu.make_async_copy(w_ada_hbm.at[ada_layer, :, pl.ds(ada_col, ada_w.shape[1])], ada_w, load_sem.at[0])
    ada_copy.start()
    fa_copy = pltpu.make_async_copy(w_fa_hbm.at[:, pl.ds(fa_col, fa_w.shape[1])], fa_w, load_sem.at[1])
    fa_copy.start()

    def w_copy(which, layer):
        src, dst = ((w_qkv_hbm, qkv_w), (w_o_hbm, o_w), (w_up_hbm, up_w), (w_down_hbm, down_w))[which]
        return pltpu.make_async_copy(src.at[layer], dst, w_sem.at[which])

    w_copy(0, 0).start()
    old_copy = pltpu.make_async_copy(old_hbm, kv.at[0], load_sem.at[2])
    old_copy.start()
    for which in range(1, 4):
        w_copy(which, 0).start()

    barrier = pltpu.get_barrier_semaphore()
    for k in range(1, chips):
        pl.semaphore_signal(barrier, inc=1, device_id=chip_dev((g + k) % chips, c), device_id_type=MESH)
    for k in range(chips_y):
        pl.semaphore_signal(barrier, inc=1, device_id=(dp, (y + k) % chips_y, 2 * x + (1 - c)), device_id_type=MESH)
    pl.semaphore_wait(barrier, chips - 1 + chips_y)

    aligned = c == y % 2
    give = 2 * (1 - c) + j_own

    def give_copies():
        return (pltpu.make_async_remote_copy(latent_ref.at[give], lat_in, in_ss.at[0], in_rs.at[0], device_id=partner, device_id_type=MESH),
                pltpu.make_async_remote_copy(pos_ref.at[give], pos_in, in_ss.at[1], in_rs.at[1], device_id=partner, device_id_type=MESH))

    @pl.when(aligned)
    def _():
        for copy in give_copies():
            copy.start()
        lat_s[...] = latent_ref[patch]
        pos_s[...] = pos_ref[patch]

    cond = cond_ref[...].astype(jnp.float32)
    act = (cond * jax.nn.sigmoid(cond)).astype(jnp.bfloat16)
    ada_copy.wait()
    ada_res = jnp.dot(act, ada_w[...], preferred_element_type=jnp.float32)
    fa_copy.wait()
    fa_res = jnp.dot(act, fa_w[...], preferred_element_type=jnp.float32)
    for t in range(2):
        for i in range(ada_tiles):
            ada_msg[t * ada_tiles + i:t * ada_tiles + i + 1, :] = ada_res[t:t + 1, i * LANES:(i + 1) * LANES]
        for i in range(fa_tiles):
            row = 2 * ada_tiles + t * fa_tiles + i
            ada_msg[row:row + 1, :] = fa_res[t:t + 1, i * LANES:(i + 1) * LANES]

    def ada_send(k):
        dest = (g + k) % chips
        return pltpu.make_async_remote_copy(ada_msg, ada_in.at[g], ada_ss.at[dest], ada_rs.at[g], device_id=chip_dev(dest, c), device_id_type=MESH)

    def ada_recv(k):
        src = (g + k) % chips
        return pltpu.make_async_remote_copy(ada_msg, ada_in.at[src], ada_ss.at[src], ada_rs.at[src], device_id=chip_dev(src, c), device_id_type=MESH)

    for k in range(1, chips):
        ada_send(k).start()
    ada_in[g] = ada_msg[...]
    bias_s[...] = b_layer_ref[...].astype(jnp.float32)

    @pl.when(aligned)
    def _():
        for copy in give_copies():
            copy.wait_send()

    @pl.when(jnp.logical_not(aligned))
    def _():
        for copy in give_copies():
            copy.wait_recv()
        lat_s[...] = lat_in[...]
        pos_s[...] = pos_in[...]

    for k in range(1, chips):
        ada_recv(k).wait_recv()
    for t in range(2):
        for layer in range(layers):
            for tile in range(ada_total):
                part = min(tile // ada_tiles, parts - 1)
                first = min(ada_tiles * part, ada_total - ada_tiles)
                row = t * ada_tiles + tile - first
                cols = slice(tile * LANES, (tile + 1) * LANES)
                mod_s[t * layers + layer:t * layers + layer + 1, cols] = ada_in[layer * parts + part, row:row + 1, :] + bias_s[layer:layer + 1, cols]
        for tile in range(fa_total):
            row = 2 * ada_tiles + t * fa_tiles + tile % fa_tiles
            cols = slice(tile * LANES, (tile + 1) * LANES)
            fmod_s[t:t + 1, cols] = ada_in[tile // fa_tiles, row:row + 1, :] + b_fa_ref[0:1, cols].astype(jnp.float32)
    for k in range(1, chips):
        ada_send(k).wait_send()
    old_copy.wait()

    lane2 = lax.broadcasted_iota(jnp.int32, (1, 2 * LANES), 1)
    lane1 = lax.broadcasted_iota(jnp.int32, (1, LANES), 1)
    factor = LOG2_E * head_dim ** -0.5
    tiles = width // LANES
    all_tiles = 3 * tiles

    def window(col, place):
        tile = min(col // LANES, all_tiles - 2)
        shift = (place - (col - tile * LANES)) % (2 * LANES)
        part = qkv_s[:, tile * LANES:(tile + 2) * LANES]
        return pltpu.roll(part, shift, 1) if shift else part

    def layer_pass(it, carry):
        t = it // layers
        layer = it % layers
        following = (it + 1) % layers
        more = it + 1 < 2 * layers
        fresh = 1 - t
        bias = lambda lo, hi: bias_s[pl.ds(layer, 1), lo * width:hi * width]
        mod = lambda i: mod_s[pl.ds(it, 1), i * width:(i + 1) * width]

        @pl.when(layer == 0)
        def _():
            emb = jnp.dot(lat_s[...].astype(jnp.bfloat16), w_in_ref[...], preferred_element_type=jnp.float32)
            hid_s[...] = (emb + pos_s[...].astype(jnp.float32)).astype(jnp.bfloat16)

        normed = (normalize(hid_s[...].astype(jnp.float32)) * (1.0 + mod(0)) + mod(1)).astype(jnp.bfloat16)
        w_copy(0, layer).wait()
        for i in (1, 2, 0):
            cols = slice(i * width, (i + 1) * width)
            part = jnp.dot(normed, qkv_w[:, cols], preferred_element_type=jnp.float32) + bias(6 + i, 7 + i)
            qkv_s[:, cols] = part.astype(jnp.bfloat16).astype(jnp.float32)

        @pl.when(more)
        def _():
            w_copy(0, following).start()

        for head in range(heads):
            at = head * head_dim
            block = jnp.where(lane2 < head_dim, window(width + at, 0),
                              jnp.where(lane2 < 2 * head_dim, window(2 * width + at, head_dim), window(at, 2 * head_dim)))
            msg[head] = block.astype(jnp.bfloat16)

        def qkv_send(k):
            dest = (g + k) % chips
            return pltpu.make_async_remote_copy(msg.at[dest], kv.at[fresh, layer, pl.ds(row_own, block_rows), :], qkv_ss.at[dest], qkv_rs.at[g], device_id=chip_dev(dest, c), device_id_type=MESH)

        def qkv_recv(k):
            src = (g + k) % chips
            return pltpu.make_async_remote_copy(msg.at[src], kv.at[fresh, layer, pl.ds(half_row(src), block_rows), :], qkv_ss.at[src], qkv_rs.at[src], device_id=chip_dev(src, c), device_id_type=MESH)

        for k in range(1, chips):
            qkv_send(k).start()
        kv[fresh, layer, pl.ds(row_own, block_rows), :] = msg[g]
        for k in range(1, chips):
            qkv_recv(k).wait_recv()

        def forward():
            rows = pl.ds(pl.multiple_of(c * half_rows, half_rows), half_rows)
            return pltpu.make_async_remote_copy(kv.at[fresh, layer, rows, :], kv.at[fresh, layer, rows, :], fwd_ss.at[layer], fwd_rs.at[layer], device_id=partner, device_id_type=MESH)

        def forwarded(slot):
            rows = pl.ds(pl.multiple_of((1 - c) * half_rows, half_rows), half_rows)
            return pltpu.make_async_remote_copy(kv.at[slot, layer, rows, :], kv.at[slot, layer, rows, :], fwd_ss.at[layer], fwd_rs.at[layer], device_id=partner, device_id_type=MESH)

        @pl.when(jnp.logical_and(c == 0, t == 1))
        def _():
            forwarded(1).wait_recv()

        @pl.when(c == 0)
        def _():
            forward().start()

        @pl.when(c == 1)
        def _():
            forwarded(fresh).wait_recv()

        for j in range(2):
            p = 2 * c + j
            q_rows = pl.ds(pl.multiple_of(p * patch_rows, patch_rows), patch_rows)
            q_part = pltpu.roll(kv[fresh, layer, q_rows, LANES:].astype(jnp.float32), 2 * LANES - 2 * head_dim, 1)
            q_part = jnp.where(lane1 < head_dim, q_part, 0.0).astype(jnp.bfloat16)
            slots = [jnp.where(kp <= p, fresh, 1 - fresh) for kp in range(patches)]
            scores = jnp.concatenate(
                [lax.dot_general(q_part, kv[slots[kp], layer, kp * patch_rows:(kp + 1) * patch_rows, :LANES], (((1,), (1,)), ((), ())), preferred_element_type=jnp.float32)
                 for kp in range(patches)], axis=1)
            top = jnp.max(scores, axis=-1, keepdims=True)
            e = jnp.exp2((scores - top) * factor)
            prob = (e * (1.0 / jnp.sum(e, axis=-1, keepdims=True))).astype(jnp.bfloat16)
            o = None
            for kp in range(patches):
                term = jnp.dot(prob[:, kp * patch_rows:(kp + 1) * patch_rows], kv[slots[kp], layer, kp * patch_rows:(kp + 1) * patch_rows, :], preferred_element_type=jnp.float32)
                o = term if o is None else o + term
            o_msg[j * patch_rows:(j + 1) * patch_rows, :] = pltpu.roll(o, 2 * LANES - head_dim, 1)[:, :LANES].astype(jnp.bfloat16)

        def o_send(k):
            dest = (g + k) % chips
            rows = pl.ds(pl.multiple_of(local_row(dest), block_rows), block_rows)
            return pltpu.make_async_remote_copy(o_msg.at[rows, :], o_in.at[g], o_ss.at[dest], o_rs.at[g], device_id=chip_dev(dest, c), device_id_type=MESH)

        def o_recv(k):
            src = (g + k) % chips
            return pltpu.make_async_remote_copy(o_msg.at[pl.ds(0, block_rows), :], o_in.at[src], o_ss.at[src], o_rs.at[src], device_id=chip_dev(src, c), device_id_type=MESH)

        for k in range(1, chips):
            o_send(k).start()
        o_in[g] = o_msg[pl.ds(pl.multiple_of(local_row(g), block_rows), block_rows), :]

        @pl.when(jnp.logical_and(c == 1, t == 0))
        def _():
            forward().start()

        for k in range(1, chips):
            o_recv(k).wait_recv()

        pieces = [None] * tiles
        for head in range(heads):
            at = head * head_dim
            tile, off = at // LANES, at % LANES
            part = o_in[head].astype(jnp.float32)
            if off:
                part = pltpu.roll(part, off, 1)
            pieces[tile] = part if pieces[tile] is None else jnp.where(lane1 >= off, part, pieces[tile])
            if off + head_dim > LANES:
                pieces[tile + 1] = part
        attn = jnp.concatenate(pieces, axis=1).astype(jnp.bfloat16)
        w_copy(1, layer).wait()
        proj = jnp.dot(attn, o_w[...], preferred_element_type=jnp.float32) + bias(9, 10)

        @pl.when(more)
        def _():
            w_copy(1, following).start()

        residual = hid_s[...].astype(jnp.float32) + mod(2) * proj
        mlp_in = (normalize(residual) * (1.0 + mod(3)) + mod(4)).astype(jnp.bfloat16)
        w_copy(2, layer).wait()
        for i in range(4):
            cols = slice(i * width, (i + 1) * width)
            up = jnp.dot(mlp_in, up_w[:, cols], preferred_element_type=jnp.float32) + bias(10 + i, 11 + i)
            mid_s[:, cols] = jax.nn.gelu(up, approximate=True).astype(jnp.bfloat16)

        @pl.when(more)
        def _():
            w_copy(2, following).start()

        w_copy(3, layer).wait()
        down = jnp.dot(mid_s[...], down_w[...], preferred_element_type=jnp.float32) + bias(14, 15)
        hid_s[...] = (residual + mod(5) * down).astype(jnp.bfloat16)

        @pl.when(more)
        def _():
            w_copy(3, following).start()

        @pl.when(layer == layers - 1)
        def _():
            scale_out = fmod_s[pl.ds(t, 1), :width]
            shift_out = fmod_s[pl.ds(t, 1), width:]
            out_rows = (normalize(hid_s[...].astype(jnp.float32)) * (1.0 + scale_out) + shift_out).astype(jnp.bfloat16)
            velocity = jnp.dot(out_rows, w_out_ref[...], preferred_element_type=jnp.float32)
            lat_s[...] = lat_s[...] + step_ref[t] * velocity

        for k in range(1, chips):
            qkv_send(k).wait_send()
            o_send(k).wait_send()

        @pl.when(jnp.logical_or(c == 0, t == 0))
        def _():
            forward().wait_send()

        return carry

    lax.fori_loop(0, 2 * layers, layer_pass, 0)

    home = 2 * x + y % 2

    def out_send(cy):
        return pltpu.make_async_remote_copy(lat_s, out_in.at[patch], out_ss.at[cy], out_rs.at[patch], device_id=(dp, cy, home), device_id_type=MESH)

    def is_self(cy):
        return jnp.logical_and(cy == y, aligned)

    for k in range(chips_y):
        cy = (y + k) % chips_y

        @pl.when(jnp.logical_not(is_self(cy)))
        def _():
            out_send(cy).start()

    @pl.when(aligned)
    def _():
        out_in[patch] = lat_s[...]

    for p in range(patches):
        @pl.when(jnp.logical_not(jnp.logical_and(aligned, patch == p)))
        def _():
            pltpu.make_async_remote_copy(lat_s, out_in.at[p], out_ss.at[p], out_rs.at[p], device_id=(dp, y, home), device_id_type=MESH).wait_recv()
    out_ref[...] = out_in[...]
    for k in range(chips_y):
        cy = (y + k) % chips_y

        @pl.when(jnp.logical_not(is_self(cy)))
        def _():
            out_send(cy).wait_send()


def solution(mesh):
    chips_y = mesh.shape["pp"]
    chips_x = mesh.shape["sp"] // 2
    chips = chips_x * chips_y
    row_spec = P("dp", "sp", None)
    full_spec = P()
    buf_spec = P("dp", None, None, None)
    in_specs = (row_spec, P(None, "sp", None), P("dp", None), P("dp"), full_spec, full_spec, full_spec, full_spec, full_spec, full_spec, full_spec, full_spec, full_spec, full_spec, buf_spec, buf_spec)

    def device_fn(latent_in, pos_embed, condition, step_size, w_in, w_ada, w_qkv, w_o, w_up, w_down, b_layer, w_fa, b_fa, w_out, k_old, v_old):
        patches, block_rows, latent_dim = latent_in.shape
        layers, width = w_qkv.shape[:2]
        tokens, heads, head_dim = k_old.shape[1:]
        my_head = lax.axis_index("pp") * chips_x + lax.axis_index("sp") // 2
        k_head = lax.dynamic_index_in_dim(k_old, my_head, axis=2, keepdims=False)
        v_head = lax.dynamic_index_in_dim(v_old, my_head, axis=2, keepdims=False)
        old_kv = jnp.concatenate([k_head, v_head, jnp.zeros((layers, tokens, 2 * LANES - 2 * head_dim), k_old.dtype)], axis=-1)
        parts = chips // layers
        ada_tiles = -(-(w_ada.shape[2] // LANES) // parts)
        fa_tiles = -(-(w_fa.shape[1] // LANES) // chips)
        ada_rows = 2 * (ada_tiles + fa_tiles)
        half_rows = 2 * block_rows * 2 * chips_x
        dims = (chips_x, chips_y, layers, patches, block_rows, width, heads, head_dim)
        bf16, f32 = jnp.bfloat16, jnp.float32
        vmem = pl.BlockSpec(memory_space=pltpu.VMEM)
        hbm = pl.BlockSpec(memory_space=pl.ANY)
        dma = pltpu.SemaphoreType.DMA
        return pl.pallas_call(
            functools.partial(kernel, dims),
            out_shape=jax.ShapeDtypeStruct(latent_in.shape, f32),
            in_specs=[vmem, vmem, vmem, pl.BlockSpec(memory_space=pltpu.SMEM), vmem, vmem, vmem, vmem] + [hbm] * 7,
            out_specs=vmem,
            scratch_shapes=[
                pltpu.VMEM((width, ada_tiles * LANES), bf16),
                pltpu.VMEM((width, fa_tiles * LANES), bf16),
                pltpu.VMEM(w_qkv.shape[1:], bf16),
                pltpu.VMEM(w_o.shape[1:], bf16),
                pltpu.VMEM(w_up.shape[1:], bf16),
                pltpu.VMEM(w_down.shape[1:], bf16),
                pltpu.VMEM((2, layers, tokens, 2 * LANES), bf16),
                pltpu.VMEM((block_rows, 3 * width), f32),
                pltpu.VMEM((chips, block_rows, 2 * LANES), bf16),
                pltpu.VMEM((half_rows, LANES), bf16),
                pltpu.VMEM((chips, block_rows, LANES), bf16),
                pltpu.VMEM((ada_rows, LANES), f32),
                pltpu.VMEM((chips, ada_rows, LANES), f32),
                pltpu.VMEM((2 * layers, w_ada.shape[2]), f32),
                pltpu.VMEM((2, w_fa.shape[1]), f32),
                pltpu.VMEM(b_layer.shape, f32),
                pltpu.VMEM((block_rows, width), bf16),
                pltpu.VMEM((block_rows, latent_dim), f32),
                pltpu.VMEM((block_rows, width), bf16),
                pltpu.VMEM((block_rows, w_up.shape[2]), bf16),
                pltpu.VMEM((block_rows, latent_dim), f32),
                pltpu.VMEM((block_rows, width), bf16),
                pltpu.VMEM((patches, block_rows, latent_dim), f32),
                dma((4,)), dma((3,)), dma((chips,)), dma((chips,)), dma((chips,)), dma((chips,)), dma((chips,)), dma((chips,)),
                dma((layers,)), dma((layers,)), dma((2,)), dma((2,)), dma((chips_y,)), dma((patches,)),
            ],
            compiler_params=pltpu.CompilerParams(collective_id=0, has_side_effects=True, vmem_limit_bytes=60 * 1024 * 1024),
        )(latent_in, pos_embed, condition, step_size, w_in, b_layer, b_fa[None, :], w_out, old_kv, w_ada, w_fa, w_qkv, w_o, w_up, w_down)

    return jax.shard_map(device_fn, mesh=mesh, in_specs=in_specs, out_specs=row_spec, check_vma=False)
```

time: 966 us -> 190 us (0.20)
  matrix products: 353 us -> 0 us
  waiting for transfers between devices: 321 us -> 0 us
  Pallas kernels: 0 us -> 181 us
  local copies, waits for them, and re-layouts: 154 us -> 6.48 us
  other arithmetic: 53.5 us -> 2.27 us
  starting transfers between devices: 45.5 us -> 0 us
  blocking collectives: 15 us -> 0 us
  between operations: 13.2 us -> 0.07 us
    dot_general x102 -> x0, matrix products: 353 us -> none  [the longest x14 153 us: run_layer(): jnp.dot(mlp_mid, down_stage[layer_j], preferred_element_type=jnp.float32)]
    all_gather x14 -> x0, waiting for transfers between devices: 315 us -> none  [run_layer(): lax.all_gather(qkv_rows[:, model_width:], 'sp', axis=0, tiled=True)]
    pallas_call x0 -> x1, Pallas kernels: none -> 181 us  [device_fn(): pl.pallas_call(functools.partial(kernel, dims), out_shape=jax.ShapeDtypeS...]
    slice x113 -> x0, local copies, waits for them, and re-layouts: 92.6 us -> none  [the longest x28 50.7 us: run_layer(): key_new = kv_patch[:, :model_width].reshape(patch_rows, num_heads, head_dim)]
    ppermute x15 -> x0, starting transfers between devices: 45.4 us -> none  [the longest x14 44.1 us: tick_body(): sent_rows = lax.ppermute(hidden, 'pp', forward_perm)]
    dynamic_update_slice x14 -> x0, other arithmetic: 34.3 us -> none  [run_layer(): lax.dynamic_update_slice_in_dim(key_buf, jnp.where(is_valid, key_new, key...]
    dynamic_slice x18 -> x3, local copies, waits for them, and re-layouts: 30.4 us -> 2.65 us  [the longest x2 2.01 us: device_fn(): v_head = lax.dynamic_index_in_dim(v_old, my_head, axis=2, keepdims=False)]
    while x56 -> x0, local copies, waits for them, and re-layouts: 18.5 us -> none
  transfers between devices with their start and end apart: 29 -> 0, of which waited for: 28 -> 0; matrix products, arithmetic and copies ran while one was open for 3% -> 0% of each run, Pallas kernels for 0% -> 0%
where the time goes in v1:
time: 190 us
  Pallas kernels  181 us (95%)
  local copies, waits for them, and re-layouts  6.48 us (3%)
  other arithmetic  2.27 us (1%)
    pallas_call x1, Pallas kernels, device_fn(): pl.pallas_call(functools.partial(kernel, dims), out_shape=jax.ShapeDtypeS...  181 us

profile of v1, /device:TPU:97, one launch (start us, length us, event | category | flops | bytes accessed | tf_op | source)
XLA Modules:
  0.0 190.0 jit_solution(9222038236596972401)
XLA Ops:
  0.0 0.0 copy-start
  0.0 0.0 copy-start.1
  0.0 0.0 copy-start.2
  0.0 1.4 constant_dynamic-slice_fusion
  1.4 0.6 copy.17
  2.1 0.6 copy.18
  2.7 0.1 pad.2.clone
  2.8 2.3 %maximum_maximum_fusion.old_hbm = bf16[4,1024,256]{2,1,0:T(8,128)(2,1)} fusion(bf16[4,1024,72]{2,1,0:T(8,128)(2,1)S(1)} %bitcast.3, bf16[4,1024,72]{2,1,0:T(8,128)(2,1)S(1)} %bitcast.2, bf16[256]{0:T(256)(128)(2,1)S(1)} %pad.2.clone), kind=kLoop, calls=%fused_computation | loop fusion | flops 6291456 | bytes 3277312 | tf_op jit(solution)/shard_map/concatenate | solution.py:379
  5.1 0.0 copy-done
  5.1 0.9 copy.20.w_out_ref
  6.0 0.0 copy-done.1
  6.0 0.7 copy.19.latent_ref
  6.7 0.0 copy-done.2
  6.7 0.6 broadcast_in_dim.6.b_fa_ref
  7.3 181.2 %shard_map.154 = f32[4,32,16]{2,1,0:T(8,128)} custom-call(f32[4,32,16]{2,1,0:T(8,128)} %copy.19.latent_ref, bf16[4,32,1152]{2,1,0:T(8,128)(2,1)} %pos_ref.1, bf16[2,1152]{1,0:T(2,128)(2,1)} %cond_ref.1, f32[2]{0:T(128)} %step_ref.1, bf16[16,1152]{1,0:T(8,128)(2,1)} %w_in_ref.1, bf16[4,17280]{1,0:T(4,128)(2,1)} %b_layer_ref.1, ...), custom_call_target="tpu_custom_call" | custom-call | tf_op jit(solution)/shard_map/pallas_call | solution.py:390
  188.5 1.5 copy.21
  (1 shorter events, 0.0 us)
Async XLA Ops:
  0.0 5.1 %copy-start = (bf16[1152,16]{0,1:T(8,128)(2,1)S(1)}, bf16[1152,16]{0,1:T(8,128)(2,1)}, u32[]{:S(2)}) copy-start(bf16[1152,16]{0,1:T(8,128)(2,1)} %param.29) | copy-start | bytes 110596
  0.0 6.0 %copy-start.1 = (f32[4,32,16]{1,2,0:T(8,128)S(1)}, f32[4,32,16]{1,2,0:T(8,128)}, u32[]{:S(2)}) copy-start(f32[4,32,16]{1,2,0:T(8,128)} %param.16) | copy-start | bytes 24580
  0.0 6.7 %copy-start.2 = (bf16[2304]{0:T(1024)(128)(2,1)S(1)}, bf16[2304]{0:T(1024)(128)(2,1)}, u32[]{:S(2)}) copy-start(bf16[2304]{0:T(1024)(128)(2,1)} %param.28) | copy-start | bytes 13828

commit v2 on v1

v2 whole, which is shorter than its diff:
```python
import functools

import jax
import jax.numpy as jnp
from jax import lax
from jax.experimental import pallas as pl
from jax.experimental.pallas import tpu as pltpu
from jax.sharding import PartitionSpec as P

LN_EPS = 1e-6
LANES = 128
LOG2_E = 1.4426950408889634
MESH = pl.DeviceIdType.MESH


def normalize(hidden):
    mean_val = jnp.mean(hidden, axis=-1, keepdims=True)
    centered = hidden - mean_val
    var_val = jnp.mean(centered * centered, axis=-1, keepdims=True)
    return centered * lax.rsqrt(var_val + LN_EPS)


def kernel(dims, latent_ref, cond_ref, step_ref, w_in_ref, b_fa_ref, w_out_ref,
           pos_hbm, b_layer_hbm, k_hbm, v_hbm, w_ada_hbm, w_fa_hbm, w_qkv_hbm, w_o_hbm, w_up_hbm, w_down_hbm,
           out_ref,
           ada_w, fa_w, qkv_w, o_w, up_w, down_w, kv, old_s, qkv_s, msg, o_msg, o_in, ada_msg, ada_in,
           mod_s, fmod_s, bias_in, bias_s, hid_s, lat_s, pos_s, mid_s, out_in,
           w_sem, load_sem, ada_ss, ada_rs, qkv_ss, qkv_rs, o_ss, o_rs, fwd_ss, fwd_rs, out_ss, out_rs):
    (chips_x, chips_y, layers, block_rows, width, heads, head_dim) = dims
    blocks = 2 * chips_x
    patch_rows = block_rows * blocks
    half_rows = 2 * patch_rows
    members = 2 * blocks
    far_order = sorted(range(chips_x), key=lambda d: -min(d, chips_x - d))
    dp = lax.axis_index("dp")
    y = lax.axis_index("pp")
    s = lax.axis_index("sp")
    x = s // 2
    core = s % 2
    upper = y // 2
    lane_row = y % 2
    own_group = jnp.where(upper == 0, lane_row, 1 - lane_row)
    my_head = own_group * blocks + s
    row_own = pl.multiple_of(y * patch_rows + s * block_rows, block_rows)

    def group_row(group):
        return jnp.where(upper == 0, group, chips_y - 1 - group)

    def column(dx, dc):
        return 2 * ((x + dx) % chips_x) + (core + dc) % 2

    def device_row(head):
        return group_row(head // blocks)

    def dev(head):
        return (dp, device_row(head), head % blocks)

    others = [(flip, dx, dc) for flip in (1, 0) for dx in far_order for dc in (1, 0) if (flip, dx, dc) != (0, 0, 0)]

    def member(flip, dx, dc):
        return (own_group + flip) % 2 * blocks + column(dx, dc)

    partner = (dp, chips_y - 1 - y, s)

    ada_tiles = ada_w.shape[1] // LANES
    ada_total = w_ada_hbm.shape[2] // LANES
    parts = members // layers
    fa_tiles = fa_w.shape[1] // LANES
    fa_total = w_fa_hbm.shape[1] // LANES

    ada_col = pl.multiple_of(jnp.minimum(ada_tiles * (my_head % parts), ada_total - ada_tiles) * LANES, LANES)
    fa_col = pl.multiple_of(jnp.minimum(fa_tiles * my_head, fa_total - fa_tiles) * LANES, LANES)
    ada_copy = pltpu.make_async_copy(w_ada_hbm.at[my_head // parts, :, pl.ds(ada_col, ada_w.shape[1])], ada_w, load_sem.at[0])
    ada_copy.start()
    fa_copy = pltpu.make_async_copy(w_fa_hbm.at[:, pl.ds(fa_col, fa_w.shape[1])], fa_w, load_sem.at[1])
    fa_copy.start()
    bias_copy = pltpu.make_async_copy(b_layer_hbm, bias_in, load_sem.at[2])
    bias_copy.start()
    pos_copy = pltpu.make_async_copy(pos_hbm.at[y], pos_s, load_sem.at[3])
    pos_copy.start()

    def w_copy(which, layer):
        src, dst = ((w_qkv_hbm, qkv_w), (w_o_hbm, o_w), (w_up_hbm, up_w), (w_down_hbm, down_w))[which]
        return pltpu.make_async_copy(src.at[layer], dst, w_sem.at[which])

    w_copy(0, 0).start()
    k_copy = pltpu.make_async_copy(k_hbm.at[:, my_head], old_s.at[0], load_sem.at[4])
    v_copy = pltpu.make_async_copy(v_hbm.at[:, my_head], old_s.at[1], load_sem.at[5])
    k_copy.start()
    v_copy.start()
    for which in range(1, 4):
        w_copy(which, 0).start()

    barrier = pltpu.get_barrier_semaphore()
    for flip, dx, dc in others:
        pl.semaphore_signal(barrier, inc=1, device_id=dev(member(flip, dx, dc)), device_id_type=MESH)
    for k in range(2):
        pl.semaphore_signal(barrier, inc=1, device_id=(dp, (1 - upper) * 2 + k, s), device_id_type=MESH)
    pl.semaphore_wait(barrier, members + 1)

    cond = cond_ref[...].astype(jnp.float32)
    act = (cond * jax.nn.sigmoid(cond)).astype(jnp.bfloat16)
    ada_copy.wait()
    ada_res = jnp.dot(act, ada_w[...], preferred_element_type=jnp.float32)
    fa_copy.wait()
    fa_res = jnp.dot(act, fa_w[...], preferred_element_type=jnp.float32)
    for t in range(2):
        for i in range(ada_tiles):
            ada_msg[t * ada_tiles + i:t * ada_tiles + i + 1, :] = ada_res[t:t + 1, i * LANES:(i + 1) * LANES]
        for i in range(fa_tiles):
            row = 2 * ada_tiles + t * fa_tiles + i
            ada_msg[row:row + 1, :] = fa_res[t:t + 1, i * LANES:(i + 1) * LANES]

    def ada_send(other):
        dest = member(*other)
        return pltpu.make_async_remote_copy(ada_msg, ada_in.at[my_head], ada_ss.at[dest], ada_rs.at[my_head], device_id=dev(dest), device_id_type=MESH)

    def ada_recv(other):
        src = member(*other)
        return pltpu.make_async_remote_copy(ada_msg, ada_in.at[src], ada_ss.at[src], ada_rs.at[src], device_id=dev(src), device_id_type=MESH)

    for other in others:
        ada_send(other).start()
    ada_in[my_head] = ada_msg[...]
    bias_copy.wait()
    bias_s[...] = bias_in[...].astype(jnp.float32)
    lat_s[...] = latent_ref[y]
    pos_copy.wait()
    k_copy.wait()
    v_copy.wait()
    for other in others:
        ada_recv(other).wait_recv()
    for t in range(2):
        for layer in range(layers):
            for tile in range(ada_total):
                part = min(tile // ada_tiles, parts - 1)
                first = min(ada_tiles * part, ada_total - ada_tiles)
                row = t * ada_tiles + tile - first
                cols = slice(tile * LANES, (tile + 1) * LANES)
                mod_s[t * layers + layer:t * layers + layer + 1, cols] = ada_in[layer * parts + part, row:row + 1, :] + bias_s[layer:layer + 1, cols]
        for tile in range(fa_total):
            row = 2 * ada_tiles + t * fa_tiles + tile % fa_tiles
            cols = slice(tile * LANES, (tile + 1) * LANES)
            fmod_s[t:t + 1, cols] = ada_in[tile // fa_tiles, row:row + 1, :] + b_fa_ref[0:1, cols].astype(jnp.float32)
    for other in others:
        ada_send(other).wait_send()

    lane2 = lax.broadcasted_iota(jnp.int32, (1, 2 * LANES), 1)
    lane1 = lax.broadcasted_iota(jnp.int32, (1, LANES), 1)
    factor = LOG2_E * head_dim ** -0.5
    tiles = width // LANES
    group_tiles = -(-(blocks * head_dim) // LANES)

    def layer_pass(it, carry):
        t = it // layers
        layer = it % layers
        following = (it + 1) % layers
        more = it + 1 < 2 * layers
        fresh = 1 - t
        bias = lambda lo, hi: bias_s[pl.ds(layer, 1), lo * width:hi * width]
        mod = lambda i: mod_s[pl.ds(it, 1), i * width:(i + 1) * width]

        @pl.when(layer == 0)
        def _():
            emb = lax.dot_general(lat_s[...].astype(jnp.bfloat16), w_in_ref[...], (((0,), (0,)), ((), ())), preferred_element_type=jnp.float32)
            hid_s[...] = (emb + pos_s[...].astype(jnp.float32)).astype(jnp.bfloat16)

        normed = (normalize(hid_s[...].astype(jnp.float32)) * (1.0 + mod(0)) + mod(1)).astype(jnp.bfloat16)
        w_copy(0, layer).wait()

        def qkv_send(dest):
            return pltpu.make_async_remote_copy(msg.at[dest], kv.at[fresh, layer, pl.ds(row_own, block_rows), :], qkv_ss.at[dest], qkv_rs.at[my_head], device_id=dev(dest), device_id_type=MESH)

        def qkv_recv(src):
            rows = pl.ds(pl.multiple_of(device_row(src) * patch_rows + src % blocks * block_rows, block_rows), block_rows)
            return pltpu.make_async_remote_copy(msg.at[src], kv.at[fresh, layer, rows, :], qkv_ss.at[src], qkv_rs.at[src], device_id=dev(src), device_id_type=MESH)

        def make_group(group):
            first = group * blocks * head_dim // LANES
            for i in (1, 2, 0):
                lo = i * width + first * LANES
                cols = slice(lo, lo + group_tiles * LANES)
                bias_cols = slice(6 * width + cols.start, 6 * width + cols.stop)
                part = jnp.dot(normed, qkv_w[:, cols], preferred_element_type=jnp.float32) + bias_s[pl.ds(layer, 1), bias_cols]
                qkv_s[:, i * group_tiles * LANES:(i + 1) * group_tiles * LANES] = part.astype(jnp.bfloat16).astype(jnp.float32)

            def window(i, head, place):
                col = head * head_dim - first * LANES
                tile = min(col // LANES, group_tiles - 2)
                shift = (place - (col - tile * LANES)) % (2 * LANES)
                lo = (i * group_tiles + tile) * LANES
                part = qkv_s[:, lo:lo + 2 * LANES]
                return pltpu.roll(part, shift, 1) if shift else part

            for head in range(group * blocks, (group + 1) * blocks):
                block = jnp.where(lane2 < head_dim, window(1, head, 0),
                                  jnp.where(lane2 < 2 * head_dim, window(2, head, head_dim), window(0, head, 2 * head_dim)))
                msg[head] = block.astype(jnp.bfloat16)
            for dx in far_order:
                for dc in (1, 0):
                    dest = group * blocks + column(dx, dc)
                    if (dx, dc) == (0, 0):
                        @pl.when(own_group != group)
                        def _():
                            qkv_send(dest).start()

                        @pl.when(own_group == group)
                        def _():
                            kv[fresh, layer, pl.ds(row_own, block_rows), :] = msg[dest]
                    else:
                        qkv_send(dest).start()

        @pl.when(own_group == 1)
        def _():
            make_group(0)

        make_group(1)

        @pl.when(own_group == 0)
        def _():
            make_group(0)

        @pl.when(more)
        def _():
            w_copy(0, following).start()

        @pl.when(t == 0)
        def _():
            for kp in range(1, chips_y):
                @pl.when(kp > 2 * upper)
                def _():
                    rows = slice(kp * patch_rows, (kp + 1) * patch_rows)
                    stack = jnp.concatenate([old_s[0, layer, :, rows].astype(jnp.float32), old_s[1, layer, :, rows].astype(jnp.float32),
                                             jnp.zeros((2 * LANES - 2 * head_dim, patch_rows), jnp.float32)], axis=0)
                    kv[0, layer, rows, :] = stack.T.astype(jnp.bfloat16)

        for other in others:
            qkv_recv(member(*other)).wait_recv()

        def half_copy(half):
            rows = pl.ds(pl.multiple_of(half * half_rows, half_rows), half_rows)
            return pltpu.make_async_remote_copy(kv.at[fresh, layer, rows, :], kv.at[fresh, layer, rows, :], fwd_ss.at[layer], fwd_rs.at[layer], device_id=partner, device_id_type=MESH)

        def stored_copy():
            rows = pl.ds(half_rows, half_rows)
            return pltpu.make_async_remote_copy(kv.at[1, layer, rows, :], kv.at[1, layer, rows, :], fwd_ss.at[layer], fwd_rs.at[layer], device_id=partner, device_id_type=MESH)

        @pl.when(jnp.logical_and(upper == 0, t == 1))
        def _():
            stored_copy().wait_recv()

        @pl.when(upper == 0)
        def _():
            half_copy(0).start()

        @pl.when(upper == 1)
        def _():
            half_copy(0).wait_recv()

        def o_send(p, col):
            rows = pl.ds(pl.multiple_of((p % 2) * patch_rows + col * block_rows, block_rows), block_rows)
            dest = jnp.where(p == y, own_group, 1 - own_group) * blocks + col
            return pltpu.make_async_remote_copy(o_msg.at[rows, :], o_in.at[my_head], o_ss.at[dest], o_rs.at[my_head], device_id=(dp, p, col), device_id_type=MESH)

        def o_recv(src):
            return pltpu.make_async_remote_copy(o_msg.at[pl.ds(0, block_rows), :], o_in.at[src], o_ss.at[src], o_rs.at[src], device_id=dev(src), device_id_type=MESH)

        for flip in (1, 0):
            p = 2 * upper + (lane_row + flip) % 2
            q_rows = pl.ds(pl.multiple_of(p * patch_rows, patch_rows), patch_rows)
            q_part = pltpu.roll(kv[fresh, layer, q_rows, LANES:].astype(jnp.float32), 2 * LANES - 2 * head_dim, 1)
            q_part = jnp.where(lane1 < head_dim, q_part, 0.0).astype(jnp.bfloat16)
            slots = [jnp.where(kp <= p, fresh, 1 - fresh) for kp in range(chips_y)]
            scores = jnp.concatenate(
                [lax.dot_general(q_part, kv[slots[kp], layer, kp * patch_rows:(kp + 1) * patch_rows, :LANES], (((1,), (1,)), ((), ())), preferred_element_type=jnp.float32)
                 for kp in range(chips_y)], axis=1)
            top = jnp.max(scores, axis=-1, keepdims=True)
            e = jnp.exp2((scores - top) * factor)
            prob = (e * (1.0 / jnp.sum(e, axis=-1, keepdims=True))).astype(jnp.bfloat16)
            o = None
            for kp in range(chips_y):
                term = jnp.dot(prob[:, kp * patch_rows:(kp + 1) * patch_rows], kv[slots[kp], layer, kp * patch_rows:(kp + 1) * patch_rows, :], preferred_element_type=jnp.float32)
                o = term if o is None else o + term
            o_rows = pl.ds(pl.multiple_of((p % 2) * patch_rows, patch_rows), patch_rows)
            o_msg[o_rows, :] = pltpu.roll(o, 2 * LANES - head_dim, 1)[:, :LANES].astype(jnp.bfloat16)
            for dx in far_order:
                for dc in (1, 0):
                    if (flip, dx, dc) != (0, 0, 0):
                        o_send(p, column(dx, dc)).start()

        o_in[my_head] = o_msg[pl.ds(pl.multiple_of(lane_row * patch_rows + s * block_rows, block_rows), block_rows), :]

        @pl.when(jnp.logical_and(upper == 1, t == 0))
        def _():
            half_copy(1).start()

        for other in others:
            o_recv(member(*other)).wait_recv()

        pieces = [None] * tiles
        for head in range(heads):
            at = head * head_dim
            tile, off = at // LANES, at % LANES
            part = o_in[head].astype(jnp.float32)
            if off:
                part = pltpu.roll(part, off, 1)
            pieces[tile] = part if pieces[tile] is None else jnp.where(lane1 >= off, part, pieces[tile])
            if off + head_dim > LANES:
                pieces[tile + 1] = part
        attn = jnp.concatenate(pieces, axis=1).astype(jnp.bfloat16)
        w_copy(1, layer).wait()
        proj = jnp.dot(attn, o_w[...], preferred_element_type=jnp.float32) + bias(9, 10)

        @pl.when(more)
        def _():
            w_copy(1, following).start()

        residual = hid_s[...].astype(jnp.float32) + mod(2) * proj
        mlp_in = (normalize(residual) * (1.0 + mod(3)) + mod(4)).astype(jnp.bfloat16)
        w_copy(2, layer).wait()
        for i in range(4):
            cols = slice(i * width, (i + 1) * width)
            up = jnp.dot(mlp_in, up_w[:, cols], preferred_element_type=jnp.float32) + bias(10 + i, 11 + i)
            mid_s[:, cols] = jax.nn.gelu(up, approximate=True).astype(jnp.bfloat16)

        @pl.when(more)
        def _():
            w_copy(2, following).start()

        w_copy(3, layer).wait()
        down = jnp.dot(mid_s[...], down_w[...], preferred_element_type=jnp.float32) + bias(14, 15)
        hid_s[...] = (residual + mod(5) * down).astype(jnp.bfloat16)

        @pl.when(more)
        def _():
            w_copy(3, following).start()

        @pl.when(layer == layers - 1)
        def _():
            scale_out = fmod_s[pl.ds(t, 1), :width]
            shift_out = fmod_s[pl.ds(t, 1), width:]
            out_rows = (normalize(hid_s[...].astype(jnp.float32)) * (1.0 + scale_out) + shift_out).astype(jnp.bfloat16)
            velocity = lax.dot_general(w_out_ref[...], out_rows, (((1,), (1,)), ((), ())), preferred_element_type=jnp.float32)
            lat_s[...] = lat_s[...] + step_ref[t] * velocity

        for other in others:
            qkv_send(member(*other)).wait_send()
            flip, dx, dc = other
            o_send(2 * upper + (lane_row + flip) % 2, column(dx, dc)).wait_send()

        @pl.when(upper == 0)
        def _():
            half_copy(0).wait_send()

        @pl.when(jnp.logical_and(upper == 1, t == 0))
        def _():
            half_copy(1).wait_send()

        return carry

    lax.fori_loop(0, 2 * layers, layer_pass, 0)

    def out_send(k):
        row = (y + k) % chips_y
        return pltpu.make_async_remote_copy(lat_s, out_in.at[y], out_ss.at[row], out_rs.at[y], device_id=(dp, row, s), device_id_type=MESH)

    def out_recv(k):
        row = (y + k) % chips_y
        return pltpu.make_async_remote_copy(lat_s, out_in.at[row], out_ss.at[row], out_rs.at[row], device_id=(dp, row, s), device_id_type=MESH)

    for k in range(1, chips_y):
        out_send(k).start()
    out_in[y] = lat_s[...]
    for k in range(1, chips_y):
        out_recv(k).wait_recv()
    out_ref[...] = out_in[...]
    for k in range(1, chips_y):
        out_send(k).wait_send()


def solution(mesh):
    chips_y = mesh.shape["pp"]
    chips_x = mesh.shape["sp"] // 2
    row_spec = P("dp", "sp", None)
    full_spec = P()
    buf_spec = P("dp", None, None, None)
    in_specs = (row_spec, P(None, "sp", None), P("dp", None), P("dp"), full_spec, full_spec, full_spec, full_spec, full_spec, full_spec, full_spec, full_spec, full_spec, full_spec, buf_spec, buf_spec)

    def device_fn(latent_in, pos_embed, condition, step_size, w_in, w_ada, w_qkv, w_o, w_up, w_down, b_layer, w_fa, b_fa, w_out, k_old, v_old):
        patches, block_rows, latent_dim = latent_in.shape
        layers, width = w_qkv.shape[:2]
        tokens, heads, head_dim = k_old.shape[1:]
        members = 4 * chips_x
        parts = members // layers
        ada_tiles = -(-(w_ada.shape[2] // LANES) // parts)
        fa_tiles = -(-(w_fa.shape[1] // LANES) // members)
        ada_rows = 2 * (ada_tiles + fa_tiles)
        half_rows = 2 * block_rows * 2 * chips_x
        group_cols = -(-(heads // 2 * head_dim) // LANES) * LANES
        dims = (chips_x, chips_y, layers, block_rows, width, heads, head_dim)
        bf16, f32 = jnp.bfloat16, jnp.float32
        vmem = pl.BlockSpec(memory_space=pltpu.VMEM)
        hbm = pl.BlockSpec(memory_space=pl.ANY)
        dma = pltpu.SemaphoreType.DMA
        latent_t = jnp.transpose(latent_in, (0, 2, 1))
        k_t = jnp.transpose(k_old, (0, 2, 3, 1))
        v_t = jnp.transpose(v_old, (0, 2, 3, 1))
        result = pl.pallas_call(
            functools.partial(kernel, dims),
            out_shape=jax.ShapeDtypeStruct(latent_t.shape, f32),
            in_specs=[vmem, vmem, pl.BlockSpec(memory_space=pltpu.SMEM), vmem, vmem, vmem] + [hbm] * 10,
            out_specs=vmem,
            scratch_shapes=[
                pltpu.VMEM((width, ada_tiles * LANES), bf16),
                pltpu.VMEM((width, fa_tiles * LANES), bf16),
                pltpu.VMEM(w_qkv.shape[1:], bf16),
                pltpu.VMEM(w_o.shape[1:], bf16),
                pltpu.VMEM(w_up.shape[1:], bf16),
                pltpu.VMEM(w_down.shape[1:], bf16),
                pltpu.VMEM((2, layers, tokens, 2 * LANES), bf16),
                pltpu.VMEM((2, layers, head_dim, tokens), bf16),
                pltpu.VMEM((block_rows, 3 * group_cols), f32),
                pltpu.VMEM((members, block_rows, 2 * LANES), bf16),
                pltpu.VMEM((half_rows, LANES), bf16),
                pltpu.VMEM((members, block_rows, LANES), bf16),
                pltpu.VMEM((ada_rows, LANES), f32),
                pltpu.VMEM((members, ada_rows, LANES), f32),
                pltpu.VMEM((2 * layers, w_ada.shape[2]), f32),
                pltpu.VMEM((2, w_fa.shape[1]), f32),
                pltpu.VMEM(b_layer.shape, bf16),
                pltpu.VMEM(b_layer.shape, f32),
                pltpu.VMEM((block_rows, width), bf16),
                pltpu.VMEM((latent_dim, block_rows), f32),
                pltpu.VMEM((block_rows, width), bf16),
                pltpu.VMEM((block_rows, w_up.shape[2]), bf16),
                pltpu.VMEM((patches, latent_dim, block_rows), f32),
                dma((4,)), dma((6,)), dma((members,)), dma((members,)), dma((members,)), dma((members,)), dma((members,)), dma((members,)),
                dma((layers,)), dma((layers,)), dma((chips_y,)), dma((chips_y,)),
            ],
            compiler_params=pltpu.CompilerParams(collective_id=0, has_side_effects=True, vmem_limit_bytes=60 * 1024 * 1024),
        )(latent_t, condition, step_size, w_in, b_fa[None, :], w_out.T, pos_embed, b_layer, k_t, v_t, w_ada, w_fa, w_qkv, w_o, w_up, w_down)
        return jnp.transpose(result, (0, 2, 1))

    return jax.shard_map(device_fn, mesh=mesh, in_specs=in_specs, out_specs=row_spec, check_vma=False)
```

time: 190 us -> 167 us (0.88)
  Pallas kernels: 181 us -> 165 us
  local copies, waits for them, and re-layouts: 6.48 us -> 2.67 us
  other arithmetic: 2.27 us -> 0 us
    pallas_call x1, Pallas kernels: 181 us -> 165 us  [device_fn(): pl.pallas_call(functools.partial(kernel, dims), out_shape=jax.ShapeDtypeS...]
    dynamic_slice x3 -> x0, local copies, waits for them, and re-layouts: 2.65 us -> none  [the longest x2 2.01 us: device_fn(): v_head = lax.dynamic_index_in_dim(v_old, my_head, axis=2, keepdims=False)]
    concatenate x1 -> x0, other arithmetic: 2.27 us -> none  [device_fn(): jnp.concatenate([k_head, v_head, jnp.zeros((layers, tokens, 2 * LANES - 2...]
where the time goes in v2:
time: 167 us
  Pallas kernels  165 us (99%)
  local copies, waits for them, and re-layouts  2.67 us (2%)
    pallas_call x1, Pallas kernels, device_fn(): pl.pallas_call(functools.partial(kernel, dims), out_shape=jax.ShapeDtypeS...  165 us

profile of v2, /device:TPU:97, one launch (start us, length us, event | category | flops | bytes accessed | tf_op | source)
XLA Modules:
  0.0 167.3 jit_solution(11749224824663260535)
XLA Ops:
  0.0 1.3 broadcast_in_dim.3.b_fa_ref
  1.3 164.6 %shard_map.154 = f32[4,16,32]{2,1,0:T(8,128)} custom-call(f32[4,16,32]{2,1,0:T(8,128)} %bitcast.9, bf16[2,1152]{1,0:T(2,128)(2,1)} %cond_ref.1, f32[2]{0:T(128)} %step_ref.1, bf16[16,1152]{1,0:T(8,128)(2,1)} %w_in_ref.1, bf16[1,2304]{1,0:T(2,128)(2,1)} %broadcast_in_dim.3.b_fa_ref, bf16[16,1152]{1,0:T(8,128)(2,1)} %bitcast.8, bf16[4,32,1152]{2,1,0:T(8,128)(2,1)} %pos_hbm.1, ...), custom_call_target="tpu_custom_call" | custom-call | tf_op jit(solution)/shard_map/pallas_call | solution.py:408
  165.9 1.4 copy.18

commit v3 on v2

v3 whole, which is shorter than its diff:
```python
import functools

import jax
import jax.numpy as jnp
from jax import lax
from jax.experimental import pallas as pl
from jax.experimental.pallas import tpu as pltpu
from jax.sharding import PartitionSpec as P

LN_EPS = 1e-6
LANES = 128
LOG2_E = 1.4426950408889634
MESH = pl.DeviceIdType.MESH


def normalize(hidden):
    mean_val = jnp.mean(hidden, axis=-1, keepdims=True)
    centered = hidden - mean_val
    var_val = jnp.mean(centered * centered, axis=-1, keepdims=True)
    return centered * lax.rsqrt(var_val + LN_EPS)


def kernel(dims, cond_ref, step_ref, w_in_ref, b_fa_ref, w_out_ref,
           latent_hbm, pos_hbm, b_layer_hbm, k_hbm, v_hbm, w_ada_hbm, w_fa_hbm, w_qkv_hbm, w_o_hbm, w_up_hbm, w_down_hbm,
           out_ref,
           ada_w, fa_w, qkv_w, o_w, up_w, down_w, kv, old_s, msg, o_msg, o_in, first_msg, first_in, ada_msg, ada_in,
           mod_s, fmod_s, bias_in, bias_s, hid_s, lat_s, pos_s,
           w_sem, load_sem, first_ss, first_rs, ada_ss, ada_rs, qkv_ss, qkv_rs, o_ss, o_rs, fwd_ss, fwd_rs, out_ss, out_rs):
    (chips_x, chips_y, layers, block_rows, width, heads, head_dim) = dims
    blocks = 2 * chips_x
    patch_rows = block_rows * blocks
    half_rows = 2 * patch_rows
    members = 2 * blocks
    far_order = sorted(range(chips_x), key=lambda d: -min(d, chips_x - d))
    dp = lax.axis_index("dp")
    y = lax.axis_index("pp")
    s = lax.axis_index("sp")
    x = s // 2
    core = s % 2
    upper = y // 2
    lane_row = y % 2
    own_group = jnp.where(upper == 0, lane_row, 1 - lane_row)
    my_head = own_group * blocks + s
    row_own = pl.multiple_of(y * patch_rows + s * block_rows, block_rows)

    def group_row(group):
        return jnp.where(upper == 0, group, chips_y - 1 - group)

    def column(dx, dc):
        return 2 * ((x + dx) % chips_x) + (core + dc) % 2

    def device_row(head):
        return group_row(head // blocks)

    def dev(head):
        return (dp, device_row(head), head % blocks)

    others = [(flip, dx, dc) for flip in (1, 0) for dx in far_order for dc in (1, 0) if (flip, dx, dc) != (0, 0, 0)]

    def member(flip, dx, dc):
        return (own_group + flip) % 2 * blocks + column(dx, dc)

    partner = (dp, chips_y - 1 - y, s)

    ada_tiles = ada_w.shape[2] // LANES
    ada_total = w_ada_hbm.shape[2] // LANES
    fa_tiles = fa_w.shape[1] // LANES
    fa_total = w_fa_hbm.shape[1] // LANES

    ada_col = pl.multiple_of(jnp.minimum(ada_tiles * my_head, ada_total - ada_tiles) * LANES, LANES)
    fa_col = pl.multiple_of(jnp.minimum(fa_tiles * my_head, fa_total - fa_tiles) * LANES, LANES)
    ada_cols = pl.ds(ada_col, ada_w.shape[2])
    ada_copy = pltpu.make_async_copy(w_ada_hbm.at[0, :, ada_cols], ada_w.at[0], load_sem.at[0])
    ada_copy.start()
    rest_copy = pltpu.make_async_copy(w_ada_hbm.at[1:, :, ada_cols], ada_w.at[1:], load_sem.at[6])
    rest_copy.start()
    fa_copy = pltpu.make_async_copy(w_fa_hbm.at[:, pl.ds(fa_col, fa_w.shape[1])], fa_w, load_sem.at[1])
    fa_copy.start()
    bias_copy = pltpu.make_async_copy(b_layer_hbm, bias_in, load_sem.at[2])
    bias_copy.start()
    pos_copy = pltpu.make_async_copy(pos_hbm.at[y], pos_s, load_sem.at[3])
    pos_copy.start()
    lat_copy = pltpu.make_async_copy(latent_hbm.at[y], lat_s, load_sem.at[7])
    lat_copy.start()

    def w_copy(which, layer):
        src, dst = ((w_qkv_hbm, qkv_w), (w_o_hbm, o_w), (w_up_hbm, up_w), (w_down_hbm, down_w))[which]
        return pltpu.make_async_copy(src.at[layer], dst, w_sem.at[which])

    k_copy = pltpu.make_async_copy(k_hbm.at[:, my_head], old_s.at[0], load_sem.at[4])
    v_copy = pltpu.make_async_copy(v_hbm.at[:, my_head], old_s.at[1], load_sem.at[5])

    barrier = pltpu.get_barrier_semaphore()
    for flip, dx, dc in others:
        pl.semaphore_signal(barrier, inc=1, device_id=dev(member(flip, dx, dc)), device_id_type=MESH)
    for k in range(2):
        pl.semaphore_signal(barrier, inc=1, device_id=(dp, (1 - upper) * 2 + k, s), device_id_type=MESH)

    cond = cond_ref[...].astype(jnp.float32)
    act = (cond * jax.nn.sigmoid(cond)).astype(jnp.bfloat16)

    def put_rows(msg_ref, row, value, count):
        for t in range(2):
            for i in range(count):
                at = row + t * count + i
                msg_ref[at:at + 1, :] = value[t:t + 1, i * LANES:(i + 1) * LANES]

    ada_copy.wait()
    w_copy(0, 0).start()
    put_rows(first_msg, 0, jnp.dot(act, ada_w[0], preferred_element_type=jnp.float32), ada_tiles)

    def first_copy(other, src_side):
        peer = member(*other)
        slot = peer if src_side else my_head
        return pltpu.make_async_remote_copy(first_msg, first_in.at[slot], first_ss.at[peer], first_rs.at[slot], device_id=dev(peer), device_id_type=MESH)

    def late_copy(other, src_side):
        peer = member(*other)
        slot = peer if src_side else my_head
        return pltpu.make_async_remote_copy(ada_msg, ada_in.at[slot], ada_ss.at[peer], ada_rs.at[slot], device_id=dev(peer), device_id_type=MESH)

    pl.semaphore_wait(barrier, members + 1)
    for other in others:
        first_copy(other, False).start()
    first_in[my_head] = first_msg[...]
    rest_copy.wait()
    for layer in range(1, layers):
        put_rows(ada_msg, (layer - 1) * 2 * ada_tiles, jnp.dot(act, ada_w[layer], preferred_element_type=jnp.float32), ada_tiles)
    fa_copy.wait()
    put_rows(ada_msg, (layers - 1) * 2 * ada_tiles, jnp.dot(act, fa_w[...], preferred_element_type=jnp.float32), fa_tiles)
    for other in others:
        late_copy(other, False).start()
    ada_in[my_head] = ada_msg[...]
    k_copy.start()
    v_copy.start()
    for which in range(1, 4):
        w_copy(which, 0).start()
    bias_copy.wait()
    bias_s[...] = bias_in[...].astype(jnp.float32)
    lat_copy.wait()
    pos_copy.wait()

    def take_rows(in_ref, base, layer):
        for t in range(2):
            for tile in range(ada_total):
                part = min(tile // ada_tiles, -(-ada_total // ada_tiles) - 1)
                first = min(ada_tiles * part, ada_total - ada_tiles)
                row = base + t * ada_tiles + tile - first
                cols = slice(tile * LANES, (tile + 1) * LANES)
                mod_s[t * layers + layer:t * layers + layer + 1, cols] = in_ref[part, row:row + 1, :] + bias_s[layer:layer + 1, cols]

    for other in others:
        first_copy(other, True).wait_recv()
    take_rows(first_in, 0, 0)

    lane2 = lax.broadcasted_iota(jnp.int32, (1, 2 * LANES), 1)
    lane1 = lax.broadcasted_iota(jnp.int32, (1, LANES), 1)
    factor = LOG2_E * head_dim ** -0.5
    tiles = width // LANES
    group_tiles = -(-(blocks * head_dim) // LANES)

    def layer_pass(it, carry):
        t = it // layers
        layer = it % layers
        following = (it + 1) % layers
        more = it + 1 < 2 * layers
        fresh = 1 - t
        bias = lambda lo, hi: bias_s[pl.ds(layer, 1), lo * width:hi * width]
        mod = lambda i: mod_s[pl.ds(it, 1), i * width:(i + 1) * width]

        @pl.when(layer == 0)
        def _():
            emb = lax.dot_general(lat_s[...].astype(jnp.bfloat16), w_in_ref[...], (((0,), (0,)), ((), ())), preferred_element_type=jnp.float32)
            hid_s[...] = (emb + pos_s[...].astype(jnp.float32)).astype(jnp.bfloat16)

        normed = (normalize(hid_s[...].astype(jnp.float32)) * (1.0 + mod(0)) + mod(1)).astype(jnp.bfloat16)
        w_copy(0, layer).wait()

        def qkv_send(dest):
            return pltpu.make_async_remote_copy(msg.at[dest], kv.at[fresh, layer, pl.ds(row_own, block_rows), :], qkv_ss.at[dest], qkv_rs.at[my_head], device_id=dev(dest), device_id_type=MESH)

        def qkv_recv(src):
            rows = pl.ds(pl.multiple_of(device_row(src) * patch_rows + src % blocks * block_rows, block_rows), block_rows)
            return pltpu.make_async_remote_copy(msg.at[src], kv.at[fresh, layer, rows, :], qkv_ss.at[src], qkv_rs.at[src], device_id=dev(src), device_id_type=MESH)

        far = 1 - own_group
        wide = group_tiles * LANES
        narrow = width - wide
        far_col = far * narrow
        near_col = (1 - far) * wide
        shift_unit = blocks * head_dim - narrow

        def columns(i, start, size):
            cols = pl.ds(pl.multiple_of(i * width + start, LANES), size)
            bias_cols = pl.ds(pl.multiple_of((6 + i) * width + start, LANES), size)
            part = jnp.dot(normed, qkv_w[:, cols], preferred_element_type=jnp.float32) + bias_s[pl.ds(layer, 1), bias_cols]
            return part.astype(jnp.bfloat16).astype(jnp.float32)

        def pack_group(group, parts):
            parts = [jnp.where(group == 1, pltpu.roll(part, wide - shift_unit, 1), part) for part in parts]

            def window(i, col, place):
                tile = min(col // LANES, group_tiles - 2)
                shift = (place - (col - tile * LANES)) % (2 * LANES)
                part = parts[i][:, tile * LANES:(tile + 2) * LANES]
                return pltpu.roll(part, shift, 1) if shift else part

            for k in range(blocks):
                col = k * head_dim
                block = jnp.where(lane2 < head_dim, window(1, col, 0),
                                  jnp.where(lane2 < 2 * head_dim, window(2, col, head_dim), window(0, col, 2 * head_dim)))
                msg[group * blocks + k] = block.astype(jnp.bfloat16)

        firsts = [columns(i, far_col, wide) for i in range(3)]
        pack_group(far, firsts)
        for dx in far_order:
            for dc in (1, 0):
                qkv_send(far * blocks + column(dx, dc)).start()
        seconds = [columns(i, near_col, narrow) for i in range(3)]
        pack_group(own_group, [jnp.where(far == 0, jnp.concatenate([first[:, narrow:], second], axis=1), jnp.concatenate([second, first[:, :wide - narrow]], axis=1))
                               for first, second in zip(firsts, seconds)])
        for dx in far_order:
            for dc in (1, 0):
                if (dx, dc) != (0, 0):
                    qkv_send(own_group * blocks + column(dx, dc)).start()
        kv[fresh, layer, pl.ds(row_own, block_rows), :] = msg[my_head]

        @pl.when(more)
        def _():
            w_copy(0, following).start()

        @pl.when(it == 0)
        def _():
            k_copy.wait()
            v_copy.wait()

        @pl.when(t == 0)
        def _():
            for kp in range(1, chips_y):
                @pl.when(kp > 2 * upper)
                def _():
                    rows = slice(kp * patch_rows, (kp + 1) * patch_rows)
                    stack = jnp.concatenate([old_s[0, layer, :, rows].astype(jnp.float32), old_s[1, layer, :, rows].astype(jnp.float32),
                                             jnp.zeros((2 * LANES - 2 * head_dim, patch_rows), jnp.float32)], axis=0)
                    kv[0, layer, rows, :] = stack.T.astype(jnp.bfloat16)

        for other in others:
            qkv_recv(member(*other)).wait_recv()

        def half_copy(half):
            rows = pl.ds(pl.multiple_of(half * half_rows, half_rows), half_rows)
            return pltpu.make_async_remote_copy(kv.at[fresh, layer, rows, :], kv.at[fresh, layer, rows, :], fwd_ss.at[layer], fwd_rs.at[layer], device_id=partner, device_id_type=MESH)

        def stored_copy():
            rows = pl.ds(half_rows, half_rows)
            return pltpu.make_async_remote_copy(kv.at[1, layer, rows, :], kv.at[1, layer, rows, :], fwd_ss.at[layer], fwd_rs.at[layer], device_id=partner, device_id_type=MESH)

        @pl.when(jnp.logical_and(upper == 0, t == 1))
        def _():
            stored_copy().wait_recv()

        @pl.when(upper == 0)
        def _():
            half_copy(0).start()

        @pl.when(upper == 1)
        def _():
            half_copy(0).wait_recv()

        def o_send(p, col):
            rows = pl.ds(pl.multiple_of((p % 2) * patch_rows + col * block_rows, block_rows), block_rows)
            dest = jnp.where(p == y, own_group, 1 - own_group) * blocks + col
            return pltpu.make_async_remote_copy(o_msg.at[rows, :], o_in.at[my_head], o_ss.at[dest], o_rs.at[my_head], device_id=(dp, p, col), device_id_type=MESH)

        def o_recv(src):
            return pltpu.make_async_remote_copy(o_msg.at[pl.ds(0, block_rows), :], o_in.at[src], o_ss.at[src], o_rs.at[src], device_id=dev(src), device_id_type=MESH)

        pair = 2 * block_rows

        def queries(flip, dxs):
            p = 2 * upper + (lane_row + flip) % 2
            offsets = [(x + dx) % chips_x * pair for dx in dxs]
            if len(dxs) == chips_x:
                q_part = kv[fresh, layer, pl.ds(pl.multiple_of(p * patch_rows, patch_rows), patch_rows), LANES:]
            else:
                q_part = jnp.concatenate([kv[fresh, layer, pl.ds(pl.multiple_of(p * patch_rows + at, pair), pair), LANES:] for at in offsets], axis=0)
            q_part = pltpu.roll(q_part.astype(jnp.float32), 2 * LANES - 2 * head_dim, 1)
            return jnp.where(lane1 < head_dim, q_part, 0.0).astype(jnp.bfloat16)

        def blocks_of(flip, lanes):
            p = 2 * upper + (lane_row + flip) % 2
            return [kv[jnp.where(kp <= p, fresh, 1 - fresh), layer, kp * patch_rows:(kp + 1) * patch_rows, :lanes] for kp in range(chips_y)]

        def score(flip, dxs):
            q_part = queries(flip, dxs)
            return [lax.dot_general(q_part, block, (((1,), (1,)), ((), ())), preferred_element_type=jnp.float32) for block in blocks_of(flip, LANES)]

        def probs(scores):
            scores = jnp.concatenate(scores, axis=1)
            top = jnp.max(scores, axis=-1, keepdims=True)
            e = jnp.exp2((scores - top) * factor)
            return (e * (1.0 / jnp.sum(e, axis=-1, keepdims=True))).astype(jnp.bfloat16)

        def values(flip, dxs, prob):
            p = 2 * upper + (lane_row + flip) % 2
            o = None
            for kp, block in enumerate(blocks_of(flip, 2 * LANES)):
                term = jnp.dot(prob[:, kp * patch_rows:(kp + 1) * patch_rows], block, preferred_element_type=jnp.float32)
                o = term if o is None else o + term
            o = pltpu.roll(o, 2 * LANES - head_dim, 1)[:, :LANES].astype(jnp.bfloat16)
            if len(dxs) == chips_x:
                o_msg[pl.ds(pl.multiple_of((p % 2) * patch_rows, patch_rows), patch_rows), :] = o
            else:
                for i, dx in enumerate(dxs):
                    o_msg[pl.ds(pl.multiple_of((p % 2) * patch_rows + (x + dx) % chips_x * pair, pair), pair), :] = o[i * pair:(i + 1) * pair]

        def send_rows(flip, dxs):
            p = 2 * upper + (lane_row + flip) % 2
            for dx in dxs:
                for dc in (1, 0):
                    if (flip, dx, dc) != (0, 0, 0):
                        o_send(p, column(dx, dc)).start()

        chunks = [(flip, far_order) for flip in (1, 0)]
        all_scores = [score(*chunk) for chunk in chunks]
        all_probs = [probs(scores) for scores in all_scores]
        for (flip, dxs), prob in zip(chunks, all_probs):
            values(flip, dxs, prob)
        for flip, dxs in chunks:
            send_rows(flip, dxs)

        o_in[my_head] = o_msg[pl.ds(pl.multiple_of(lane_row * patch_rows + s * block_rows, block_rows), block_rows), :]

        @pl.when(jnp.logical_and(upper == 1, t == 0))
        def _():
            half_copy(1).start()

        @pl.when(it == 0)
        def _():
            for other in others:
                late_copy(other, True).wait_recv()
            for late in range(1, layers):
                take_rows(ada_in, (late - 1) * 2 * ada_tiles, late)
            for step in range(2):
                for tile in range(fa_total):
                    row = (layers - 1) * 2 * ada_tiles + step * fa_tiles + tile % fa_tiles
                    cols = slice(tile * LANES, (tile + 1) * LANES)
                    fmod_s[step:step + 1, cols] = ada_in[tile // fa_tiles, row:row + 1, :] + b_fa_ref[cols].astype(jnp.float32).reshape(1, LANES)
            for other in others:
                first_copy(other, False).wait_send()
                late_copy(other, False).wait_send()

        for other in others:
            o_recv(member(*other)).wait_recv()

        pieces = [None] * tiles
        for head in range(heads):
            at = head * head_dim
            tile, off = at // LANES, at % LANES
            part = o_in[head].astype(jnp.float32)
            if off:
                part = pltpu.roll(part, off, 1)
            pieces[tile] = part if pieces[tile] is None else jnp.where(lane1 >= off, part, pieces[tile])
            if off + head_dim > LANES:
                pieces[tile + 1] = part
        attn = jnp.concatenate(pieces, axis=1).astype(jnp.bfloat16)
        w_copy(1, layer).wait()
        proj = jnp.dot(attn, o_w[...], preferred_element_type=jnp.float32) + bias(9, 10)

        @pl.when(more)
        def _():
            w_copy(1, following).start()

        residual = hid_s[...].astype(jnp.float32) + mod(2) * proj
        mlp_in = (normalize(residual) * (1.0 + mod(3)) + mod(4)).astype(jnp.bfloat16)
        w_copy(2, layer).wait()
        up_cols = up_w.shape[1] // 4
        w_copy(3, layer).wait()
        down = bias(14, 15)
        for i in range(4):
            cols = slice(i * up_cols, (i + 1) * up_cols)
            up_bias = bias_s[pl.ds(layer, 1), 10 * width + i * up_cols:10 * width + (i + 1) * up_cols]
            up = jnp.dot(mlp_in, up_w[:, cols], preferred_element_type=jnp.float32) + up_bias
            mid = jax.nn.gelu(up, approximate=True).astype(jnp.bfloat16)
            down = down + jnp.dot(mid, down_w[cols, :], preferred_element_type=jnp.float32)

        @pl.when(more)
        def _():
            w_copy(2, following).start()

        hid_s[...] = (residual + mod(5) * down).astype(jnp.bfloat16)

        @pl.when(more)
        def _():
            w_copy(3, following).start()

        @pl.when(layer == layers - 1)
        def _():
            scale_out = fmod_s[pl.ds(t, 1), :width]
            shift_out = fmod_s[pl.ds(t, 1), width:]
            out_rows = (normalize(hid_s[...].astype(jnp.float32)) * (1.0 + scale_out) + shift_out).astype(jnp.bfloat16)
            velocity = lax.dot_general(w_out_ref[...], out_rows, (((1,), (1,)), ((), ())), preferred_element_type=jnp.float32)
            lat_s[...] = lat_s[...] + step_ref[t] * velocity

        for other in others:
            qkv_send(member(*other)).wait_send()
            flip, dx, dc = other
            o_send(2 * upper + (lane_row + flip) % 2, column(dx, dc)).wait_send()

        @pl.when(upper == 0)
        def _():
            half_copy(0).wait_send()

        @pl.when(jnp.logical_and(upper == 1, t == 0))
        def _():
            half_copy(1).wait_send()

        return carry

    lax.fori_loop(0, 2 * layers, layer_pass, 0)

    def out_copy(k, src_side):
        row = (y + k) % chips_y
        slot = row if src_side else y
        return pltpu.make_async_remote_copy(lat_s, out_ref.at[slot], out_ss.at[row], out_rs.at[slot], device_id=(dp, row, s), device_id_type=MESH)

    for k in range(1, chips_y):
        out_copy(k, False).start()
    own_copy = pltpu.make_async_copy(lat_s, out_ref.at[y], load_sem.at[0])
    own_copy.start()
    for k in range(1, chips_y):
        out_copy(k, True).wait_recv()
    own_copy.wait()
    for k in range(1, chips_y):
        out_copy(k, False).wait_send()


def solution(mesh):
    chips_y = mesh.shape["pp"]
    chips_x = mesh.shape["sp"] // 2
    row_spec = P("dp", "sp", None)
    full_spec = P()
    buf_spec = P("dp", None, None, None)
    in_specs = (row_spec, P(None, "sp", None), P("dp", None), P("dp"), full_spec, full_spec, full_spec, full_spec, full_spec, full_spec, full_spec, full_spec, full_spec, full_spec, buf_spec, buf_spec)

    def device_fn(latent_in, pos_embed, condition, step_size, w_in, w_ada, w_qkv, w_o, w_up, w_down, b_layer, w_fa, b_fa, w_out, k_old, v_old):
        patches, block_rows, latent_dim = latent_in.shape
        layers, width = w_qkv.shape[:2]
        tokens, heads, head_dim = k_old.shape[1:]
        members = 4 * chips_x
        ada_tiles = -(-(w_ada.shape[2] // LANES) // members)
        fa_tiles = -(-(w_fa.shape[1] // LANES) // members)
        ada_rows = 2 * ((layers - 1) * ada_tiles + fa_tiles)
        half_rows = 2 * block_rows * 2 * chips_x
        dims = (chips_x, chips_y, layers, block_rows, width, heads, head_dim)
        bf16, f32 = jnp.bfloat16, jnp.float32
        vmem = pl.BlockSpec(memory_space=pltpu.VMEM)
        hbm = pl.BlockSpec(memory_space=pl.ANY)
        dma = pltpu.SemaphoreType.DMA
        latent_t = jnp.transpose(latent_in, (0, 2, 1))
        k_t = jnp.transpose(k_old, (0, 2, 3, 1))
        v_t = jnp.transpose(v_old, (0, 2, 3, 1))
        result = pl.pallas_call(
            functools.partial(kernel, dims),
            out_shape=jax.ShapeDtypeStruct(latent_t.shape, f32),
            in_specs=[vmem, pl.BlockSpec(memory_space=pltpu.SMEM), vmem, vmem, vmem] + [hbm] * 11,
            out_specs=hbm,
            scratch_shapes=[
                pltpu.VMEM((layers, width, ada_tiles * LANES), bf16),
                pltpu.VMEM((width, fa_tiles * LANES), bf16),
                pltpu.VMEM(w_qkv.shape[1:], bf16),
                pltpu.VMEM(w_o.shape[1:], bf16),
                pltpu.VMEM(w_up.shape[1:], bf16),
                pltpu.VMEM(w_down.shape[1:], bf16),
                pltpu.VMEM((2, layers, tokens, 2 * LANES), bf16),
                pltpu.VMEM((2, layers, head_dim, tokens), bf16),
                pltpu.VMEM((members, block_rows, 2 * LANES), bf16),
                pltpu.VMEM((half_rows, LANES), bf16),
                pltpu.VMEM((members, block_rows, LANES), bf16),
                pltpu.VMEM((2 * ada_tiles, LANES), f32),
                pltpu.VMEM((members, 2 * ada_tiles, LANES), f32),
                pltpu.VMEM((ada_rows, LANES), f32),
                pltpu.VMEM((members, ada_rows, LANES), f32),
                pltpu.VMEM((2 * layers, w_ada.shape[2]), f32),
                pltpu.VMEM((2, w_fa.shape[1]), f32),
                pltpu.VMEM(b_layer.shape, bf16),
                pltpu.VMEM(b_layer.shape, f32),
                pltpu.VMEM((block_rows, width), bf16),
                pltpu.VMEM((latent_dim, block_rows), f32),
                pltpu.VMEM((block_rows, width), bf16),
                dma((4,)), dma((8,)), dma((members,)), dma((members,)), dma((members,)), dma((members,)), dma((members,)), dma((members,)), dma((members,)), dma((members,)),
                dma((layers,)), dma((layers,)), dma((chips_y,)), dma((chips_y,)),
            ],
            compiler_params=pltpu.CompilerParams(collective_id=0, has_side_effects=True, vmem_limit_bytes=60 * 1024 * 1024),
        )(condition, step_size, w_in, b_fa, w_out.T, latent_t, pos_embed, b_layer, k_t, v_t, w_ada, w_fa, w_qkv, w_o, w_up, w_down)
        return jnp.transpose(result, (0, 2, 1))

    return jax.shard_map(device_fn, mesh=mesh, in_specs=in_specs, out_specs=row_spec, check_vma=False)
```

time: 167 us -> 158 us (0.946)
  Pallas kernels: 165 us -> 156 us
    pallas_call x1, Pallas kernels: 165 us -> 156 us  [device_fn(): pl.pallas_call(functools.partial(kernel, dims), out_shape=jax.ShapeDtypeS...]
where the time goes in v3:
time: 158 us
  Pallas kernels  156 us (99%)
    pallas_call x1, Pallas kernels, device_fn(): pl.pallas_call(functools.partial(kernel, dims), out_shape=jax.ShapeDtypeS...  156 us

profile of v3, /device:TPU:97, one launch (start us, length us, event | category | flops | bytes accessed | tf_op | source)
XLA Modules:
  0.0 157.6 jit_solution(12921673429740218618)
XLA Ops:
  0.0 156.2 %shard_map.154 = f32[4,16,32]{2,1,0:T(8,128)} custom-call(bf16[2,1152]{1,0:T(2,128)(2,1)} %cond_ref.1, f32[2]{0:T(128)} %step_ref.1, bf16[16,1152]{1,0:T(8,128)(2,1)} %w_in_ref.1, bf16[2304]{0:T(1024)(128)(2,1)} %b_fa_ref.1, bf16[16,1152]{1,0:T(8,128)(2,1)} %bitcast.8, f32[4,16,32]{2,1,0:T(8,128)} %bitcast.9, bf16[4,32,1152]{2,1,0:T(8,128)(2,1)} %pos_hbm.1, ...), custom_call_target="tpu_custom_call" | custom-call | tf_op jit(solution)/shard_map/pallas_call | solution.py:463
  156.3 1.4 copy.18

commit v4 on v3

--- a/solution.py
+++ b/solution.py
@@ -23,9 +23,9 @@
 def kernel(dims, cond_ref, step_ref, w_in_ref, b_fa_ref, w_out_ref,
            latent_hbm, pos_hbm, b_layer_hbm, k_hbm, v_hbm, w_ada_hbm, w_fa_hbm, w_qkv_hbm, w_o_hbm, w_up_hbm, w_down_hbm,
            out_ref,
-           ada_w, fa_w, qkv_w, o_w, up_w, down_w, kv, old_s, msg, o_msg, o_in, first_msg, first_in, ada_msg, ada_in,
+           head_w, ada_w, fa_w, qkv_w, o_w, up_w, down_w, kv, old_s, msg, o_msg, o_in, ada_msg, ada_in,
            mod_s, fmod_s, bias_in, bias_s, hid_s, lat_s, pos_s,
-           w_sem, load_sem, first_ss, first_rs, ada_ss, ada_rs, qkv_ss, qkv_rs, o_ss, o_rs, fwd_ss, fwd_rs, out_ss, out_rs):
+           w_sem, load_sem, ada_ss, ada_rs, qkv_ss, qkv_rs, o_ss, o_rs, fwd_ss, fwd_rs, out_ss, out_rs):
     (chips_x, chips_y, layers, block_rows, width, heads, head_dim) = dims
     blocks = 2 * chips_x
     patch_rows = block_rows * blocks
@@ -69,26 +69,24 @@
 
     ada_col = pl.multiple_of(jnp.minimum(ada_tiles * my_head, ada_total - ada_tiles) * LANES, LANES)
     fa_col = pl.multiple_of(jnp.minimum(fa_tiles * my_head, fa_total - fa_tiles) * LANES, LANES)
-    ada_cols = pl.ds(ada_col, ada_w.shape[2])
-    ada_copy = pltpu.make_async_copy(w_ada_hbm.at[0, :, ada_cols], ada_w.at[0], load_sem.at[0])
-    ada_copy.start()
-    rest_copy = pltpu.make_async_copy(w_ada_hbm.at[1:, :, ada_cols], ada_w.at[1:], load_sem.at[6])
-    rest_copy.start()
-    fa_copy = pltpu.make_async_copy(w_fa_hbm.at[:, pl.ds(fa_col, fa_w.shape[1])], fa_w, load_sem.at[1])
-    fa_copy.start()
+    head_copy = pltpu.make_async_copy(w_ada_hbm.at[0, :, pl.ds(0, head_w.shape[1])], head_w, load_sem.at[0])
+    head_copy.start()
     bias_copy = pltpu.make_async_copy(b_layer_hbm, bias_in, load_sem.at[2])
     bias_copy.start()
     pos_copy = pltpu.make_async_copy(pos_hbm.at[y], pos_s, load_sem.at[3])
     pos_copy.start()
     lat_copy = pltpu.make_async_copy(latent_hbm.at[y], lat_s, load_sem.at[7])
     lat_copy.start()
+    ada_copy = pltpu.make_async_copy(w_ada_hbm.at[:, :, pl.ds(ada_col, ada_w.shape[2])], ada_w, load_sem.at[6])
+    fa_copy = pltpu.make_async_copy(w_fa_hbm.at[:, pl.ds(fa_col, fa_w.shape[1])], fa_w, load_sem.at[1])
+    k_copy = pltpu.make_async_copy(k_hbm.at[:, my_head], old_s.at[0], load_sem.at[4])
+    v_copy = pltpu.make_async_copy(v_hbm.at[:, my_head], old_s.at[1], load_sem.at[5])
 
     def w_copy(which, layer):
         src, dst = ((w_qkv_hbm, qkv_w), (w_o_hbm, o_w), (w_up_hbm, up_w), (w_down_hbm, down_w))[which]
         return pltpu.make_async_copy(src.at[layer], dst, w_sem.at[which])
 
-    k_copy = pltpu.make_async_copy(k_hbm.at[:, my_head], old_s.at[0], load_sem.at[4])
-    v_copy = pltpu.make_async_copy(v_hbm.at[:, my_head], old_s.at[1], load_sem.at[5])
+    w_copy(0, 0).start()
 
     barrier = pltpu.get_barrier_semaphore()
     for flip, dx, dc in others:
@@ -96,62 +94,46 @@
     for k in range(2):
         pl.semaphore_signal(barrier, inc=1, device_id=(dp, (1 - upper) * 2 + k, s), device_id_type=MESH)
 
-    cond = cond_ref[...].astype(jnp.float32)
-    act = (cond * jax.nn.sigmoid(cond)).astype(jnp.bfloat16)
-
-    def put_rows(msg_ref, row, value, count):
+    def activation():
+        cond = cond_ref[...].astype(jnp.float32)
+        return (cond * jax.nn.sigmoid(cond)).astype(jnp.bfloat16)
+
+    def put_rows(row, value, count):
         for t in range(2):
             for i in range(count):
                 at = row + t * count + i
-                msg_ref[at:at + 1, :] = value[t:t + 1, i * LANES:(i + 1) * LANES]
-
-    ada_copy.wait()
-    w_copy(0, 0).start()
-    put_rows(first_msg, 0, jnp.dot(act, ada_w[0], preferred_element_type=jnp.float32), ada_tiles)
-
-    def first_copy(other, src_side):
-        peer = member(*other)
-        slot = peer if src_side else my_head
-        return pltpu.make_async_remote_copy(first_msg, first_in.at[slot], first_ss.at[peer], first_rs.at[slot], device_id=dev(peer), device_id_type=MESH)
-
-    def late_copy(other, src_side):
-        peer = member(*other)
-        slot = peer if src_side else my_head
-        return pltpu.make_async_remote_copy(ada_msg, ada_in.at[slot], ada_ss.at[peer], ada_rs.at[slot], device_id=dev(peer), device_id_type=MESH)
-
-    pl.semaphore_wait(barrier, members + 1)
-    for other in others:
-        first_copy(other, False).start()
-    first_in[my_head] = first_msg[...]
-    rest_copy.wait()
-    for layer in range(1, layers):
-        put_rows(ada_msg, (layer - 1) * 2 * ada_tiles, jnp.dot(act, ada_w[layer], preferred_element_type=jnp.float32), ada_tiles)
-    fa_copy.wait()
-    put_rows(ada_msg, (layers - 1) * 2 * ada_tiles, jnp.dot(act, fa_w[...], preferred_element_type=jnp.float32), fa_tiles)
-    for other in others:
-        late_copy(other, False).start()
-    ada_in[my_head] = ada_msg[...]
-    k_copy.start()
-    v_copy.start()
-    for which in range(1, 4):
-        w_copy(which, 0).start()
-    bias_copy.wait()
-    bias_s[...] = bias_in[...].astype(jnp.float32)
-    lat_copy.wait()
-    pos_copy.wait()
-
-    def take_rows(in_ref, base, layer):
+                ada_msg[at:at + 1, :] = value[t:t + 1, i * LANES:(i + 1) * LANES]
+
+    def ada_send(other):
+        dest = member(*other)
+        return pltpu.make_async_remote_copy(ada_msg, ada_in.at[my_head], ada_ss.at[dest], ada_rs.at[my_head], device_id=dev(dest), device_id_type=MESH)
+
+    def ada_recv(other):
+        src = member(*other)
+        return pltpu.make_async_remote_copy(ada_msg, ada_in.at[src], ada_ss.at[src], ada_rs.at[src], device_id=dev(src), device_id_type=MESH)
+
+    def take_rows(base, layer):
         for t in range(2):
             for tile in range(ada_total):
                 part = min(tile // ada_tiles, -(-ada_total // ada_tiles) - 1)
                 first = min(ada_tiles * part, ada_total - ada_tiles)
                 row = base + t * ada_tiles + tile - first
                 cols = slice(tile * LANES, (tile + 1) * LANES)
-                mod_s[t * layers + layer:t * layers + layer + 1, cols] = in_ref[part, row:row + 1, :] + bias_s[layer:layer + 1, cols]
-
-    for other in others:
-        first_copy(other, True).wait_recv()
-    take_rows(first_in, 0, 0)
+                mod_s[t * layers + layer:t * layers + layer + 1, cols] = ada_in[part, row:row + 1, :] + bias_s[layer:layer + 1, cols]
+
+    bias_copy.wait()
+    bias_s[...] = bias_in[...].astype(jnp.float32)
+    head_copy.wait()
+    ada_copy.start()
+    fa_copy.start()
+    k_copy.start()
+    v_copy.start()
+    head_res = jnp.dot(activation(), head_w[...], preferred_element_type=jnp.float32)
+    for t in range(2):
+        mod_s[t * layers:t * layers + 1, :2 * width] = head_res[t:t + 1] + bias_s[0:1, :2 * width]
+    lat_copy.wait()
+    pos_copy.wait()
+    pl.semaphore_wait(barrier, members + 1)
 
     lane2 = lax.broadcasted_iota(jnp.int32, (1, 2 * LANES), 1)
     lane1 = lax.broadcasted_iota(jnp.int32, (1, LANES), 1)
@@ -175,6 +157,11 @@
 
         normed = (normalize(hid_s[...].astype(jnp.float32)) * (1.0 + mod(0)) + mod(1)).astype(jnp.bfloat16)
         w_copy(0, layer).wait()
+
+        @pl.when(it == 0)
+        def _():
+            for which in range(1, 4):
+                w_copy(which, 0).start()
 
         def qkv_send(dest):
             return pltpu.make_async_remote_copy(msg.at[dest], kv.at[fresh, layer, pl.ds(row_own, block_rows), :], qkv_ss.at[dest], qkv_rs.at[my_head], device_id=dev(dest), device_id_type=MESH)
@@ -231,6 +218,15 @@
 
         @pl.when(it == 0)
         def _():
+            act = activation()
+            ada_copy.wait()
+            for part_layer in range(layers):
+                put_rows(part_layer * 2 * ada_tiles, jnp.dot(act, ada_w[part_layer], preferred_element_type=jnp.float32), ada_tiles)
+            fa_copy.wait()
+            put_rows(layers * 2 * ada_tiles, jnp.dot(act, fa_w[...], preferred_element_type=jnp.float32), fa_tiles)
+            for other in others:
+                ada_send(other).start()
+            ada_in[my_head] = ada_msg[...]
             k_copy.wait()
             v_copy.wait()
 
@@ -338,17 +334,16 @@
         @pl.when(it == 0)
         def _():
             for other in others:
-                late_copy(other, True).wait_recv()
-            for late in range(1, layers):
-                take_rows(ada_in, (late - 1) * 2 * ada_tiles, late)
+                ada_recv(other).wait_recv()
+            for late in range(layers):
+                take_rows(late * 2 * ada_tiles, late)
             for step in range(2):
                 for tile in range(fa_total):
-                    row = (layers - 1) * 2 * ada_tiles + step * fa_tiles + tile % fa_tiles
+                    row = layers * 2 * ada_tiles + step * fa_tiles + tile % fa_tiles
                     cols = slice(tile * LANES, (tile + 1) * LANES)
                     fmod_s[step:step + 1, cols] = ada_in[tile // fa_tiles, row:row + 1, :] + b_fa_ref[cols].astype(jnp.float32).reshape(1, LANES)
             for other in others:
-                first_copy(other, False).wait_send()
-                late_copy(other, False).wait_send()
+                ada_send(other).wait_send()
 
         for other in others:
             o_recv(member(*other)).wait_recv()
@@ -450,7 +445,7 @@
         members = 4 * chips_x
         ada_tiles = -(-(w_ada.shape[2] // LANES) // members)
         fa_tiles = -(-(w_fa.shape[1] // LANES) // members)
-        ada_rows = 2 * ((layers - 1) * ada_tiles + fa_tiles)
+        ada_rows = 2 * (layers * ada_tiles + fa_tiles)
         half_rows = 2 * block_rows * 2 * chips_x
         dims = (chips_x, chips_y, layers, block_rows, width, heads, head_dim)
         bf16, f32 = jnp.bfloat16, jnp.float32
@@ -466,6 +461,7 @@
             in_specs=[vmem, pl.BlockSpec(memory_space=pltpu.SMEM), vmem, vmem, vmem] + [hbm] * 11,
             out_specs=hbm,
             scratch_shapes=[
+                pltpu.VMEM((width, 2 * width), bf16),
                 pltpu.VMEM((layers, width, ada_tiles * LANES), bf16),
                 pltpu.VMEM((width, fa_tiles * LANES), bf16),
                 pltpu.VMEM(w_qkv.shape[1:], bf16),
@@ -477,8 +473,6 @@
                 pltpu.VMEM((members, block_rows, 2 * LANES), bf16),
                 pltpu.VMEM((half_rows, LANES), bf16),
                 pltpu.VMEM((members, block_rows, LANES), bf16),
-                pltpu.VMEM((2 * ada_tiles, LANES), f32),
-                pltpu.VMEM((members, 2 * ada_tiles, LANES), f32),
                 pltpu.VMEM((ada_rows, LANES), f32),
                 pltpu.VMEM((members, ada_rows, LANES), f32),
                 pltpu.VMEM((2 * layers, w_ada.shape[2]), f32),
@@ -488,7 +482,7 @@
                 pltpu.VMEM((block_rows, width), bf16),
                 pltpu.VMEM((latent_dim, block_rows), f32),
                 pltpu.VMEM((block_rows, width), bf16),
-                dma((4,)), dma((8,)), dma((members,)), dma((members,)), dma((members,)), dma((members,)), dma((members,)), dma((members,)), dma((members,)), dma((members,)),
+                dma((4,)), dma((8,)), dma((members,)), dma((members,)), dma((members,)), dma((members,)), dma((members,)), dma((members,)),
                 dma((layers,)), dma((layers,)), dma((chips_y,)), dma((chips_y,)),
             ],
             compiler_params=pltpu.CompilerParams(collective_id=0, has_side_effects=True, vmem_limit_bytes=60 * 1024 * 1024),

time: 158 us -> 154 us (0.975)
  Pallas kernels: 156 us -> 152 us
    pallas_call x1, Pallas kernels: 156 us -> 152 us  [device_fn(): pl.pallas_call(functools.partial(kernel, dims), out_shape=jax.ShapeDtypeS...]
where the time goes in v4:
time: 154 us
  Pallas kernels  152 us (99%)
    pallas_call x1, Pallas kernels, device_fn(): pl.pallas_call(functools.partial(kernel, dims), out_shape=jax.ShapeDtypeS...  152 us

profile of v4, /device:TPU:97, one launch (start us, length us, event | category | flops | bytes accessed | tf_op | source)
XLA Modules:
  0.0 153.6 jit_solution(3353605949862035002)
XLA Ops:
  0.0 152.2 %shard_map.154 = f32[4,16,32]{2,1,0:T(8,128)} custom-call(bf16[2,1152]{1,0:T(2,128)(2,1)} %cond_ref.1, f32[2]{0:T(128)} %step_ref.1, bf16[16,1152]{1,0:T(8,128)(2,1)} %w_in_ref.1, bf16[2304]{0:T(1024)(128)(2,1)} %b_fa_ref.1, bf16[16,1152]{1,0:T(8,128)(2,1)} %bitcast.8, f32[4,16,32]{2,1,0:T(8,128)} %bitcast.9, bf16[4,32,1152]{2,1,0:T(8,128)(2,1)} %pos_hbm.1, ...), custom_call_target="tpu_custom_call" | custom-call | tf_op jit(solution)/shard_map/pallas_call | solution.py:458
  152.3 1.4 copy.18

commit v5 on v4

--- a/solution.py
+++ b/solution.py
@@ -24,8 +24,8 @@
            latent_hbm, pos_hbm, b_layer_hbm, k_hbm, v_hbm, w_ada_hbm, w_fa_hbm, w_qkv_hbm, w_o_hbm, w_up_hbm, w_down_hbm,
            out_ref,
            head_w, ada_w, fa_w, qkv_w, o_w, up_w, down_w, kv, old_s, msg, o_msg, o_in, ada_msg, ada_in,
-           mod_s, fmod_s, bias_in, bias_s, hid_s, lat_s, pos_s,
-           w_sem, load_sem, ada_ss, ada_rs, qkv_ss, qkv_rs, o_ss, o_rs, fwd_ss, fwd_rs, out_ss, out_rs):
+           mod_s, fmod_s, bias_in, bias_s, hid_s, lat_s, pos_s, pack_out, pack_in,
+           w_sem, load_sem, ada_ss, ada_rs, qkv_ss, qkv_rs, o_ss, o_rs, fwd_ss, fwd_rs, out_ss, out_rs, pack_ss, pack_rs):
     (chips_x, chips_y, layers, block_rows, width, heads, head_dim) = dims
     blocks = 2 * chips_x
     patch_rows = block_rows * blocks
@@ -140,6 +140,9 @@
     factor = LOG2_E * head_dim ** -0.5
     tiles = width // LANES
     group_tiles = -(-(blocks * head_dim) // LANES)
+    rest = 2 * head_dim - LANES
+    packs = LANES // rest
+    pack_rows = half_rows // packs
 
     def layer_pass(it, carry):
         t = it // layers
@@ -243,9 +246,10 @@
         for other in others:
             qkv_recv(member(*other)).wait_recv()
 
-        def half_copy(half):
-            rows = pl.ds(pl.multiple_of(half * half_rows, half_rows), half_rows)
-            return pltpu.make_async_remote_copy(kv.at[fresh, layer, rows, :], kv.at[fresh, layer, rows, :], fwd_ss.at[layer], fwd_rs.at[layer], device_id=partner, device_id_type=MESH)
+        def lower_copies():
+            rows = pl.ds(0, half_rows)
+            return (pltpu.make_async_remote_copy(kv.at[fresh, layer, rows, pl.ds(0, LANES)], kv.at[fresh, layer, rows, pl.ds(0, LANES)], fwd_ss.at[layer], fwd_rs.at[layer], device_id=partner, device_id_type=MESH),
+                    pltpu.make_async_remote_copy(pack_out, pack_in.at[layer], pack_ss.at[layer], pack_rs.at[layer], device_id=partner, device_id_type=MESH))
 
         def stored_copy():
             rows = pl.ds(half_rows, half_rows)
@@ -257,11 +261,24 @@
 
         @pl.when(upper == 0)
         def _():
-            half_copy(0).start()
+            packed = None
+            for r in range(packs):
+                part = kv[fresh, layer, r * pack_rows:(r + 1) * pack_rows, LANES:].astype(jnp.float32)
+                if r:
+                    part = pltpu.roll(part, r * rest, 1)
+                packed = part if packed is None else jnp.where(lane1 >= r * rest, part, packed)
+            pack_out[...] = packed.astype(jnp.bfloat16)
+            for copy in lower_copies():
+                copy.start()
 
         @pl.when(upper == 1)
         def _():
-            half_copy(0).wait_recv()
+            for copy in lower_copies():
+                copy.wait_recv()
+            packed = pack_in[layer].astype(jnp.float32)
+            for r in range(packs):
+                part = pltpu.roll(packed, LANES - r * rest, 1) if r else packed
+                kv[fresh, layer, r * pack_rows:(r + 1) * pack_rows, LANES:] = part.astype(jnp.bfloat16)
 
         def o_send(p, col):
             rows = pl.ds(pl.multiple_of((p % 2) * patch_rows + col * block_rows, block_rows), block_rows)
@@ -329,7 +346,7 @@
 
         @pl.when(jnp.logical_and(upper == 1, t == 0))
         def _():
-            half_copy(1).start()
+            stored_copy().start()
 
         @pl.when(it == 0)
         def _():
@@ -404,11 +421,12 @@
 
         @pl.when(upper == 0)
         def _():
-            half_copy(0).wait_send()
+            for copy in lower_copies():
+                copy.wait_send()
 
         @pl.when(jnp.logical_and(upper == 1, t == 0))
         def _():
-            half_copy(1).wait_send()
+            stored_copy().wait_send()
 
         return carry
 
@@ -482,8 +500,10 @@
                 pltpu.VMEM((block_rows, width), bf16),
                 pltpu.VMEM((latent_dim, block_rows), f32),
                 pltpu.VMEM((block_rows, width), bf16),
+                pltpu.VMEM((half_rows * (2 * head_dim - LANES) // LANES, LANES), bf16),
+                pltpu.VMEM((layers, half_rows * (2 * head_dim - LANES) // LANES, LANES), bf16),
                 dma((4,)), dma((8,)), dma((members,)), dma((members,)), dma((members,)), dma((members,)), dma((members,)), dma((members,)),
-                dma((layers,)), dma((layers,)), dma((chips_y,)), dma((chips_y,)),
+                dma((layers,)), dma((layers,)), dma((chips_y,)), dma((chips_y,)), dma((layers,)), dma((layers,)),
             ],
             compiler_params=pltpu.CompilerParams(collective_id=0, has_side_effects=True, vmem_limit_bytes=60 * 1024 * 1024),
         )(condition, step_size, w_in, b_fa, w_out.T, latent_t, pos_embed, b_layer, k_t, v_t, w_ada, w_fa, w_qkv, w_o, w_up, w_down)

time: 154 us -> 153 us (level)
  no operation moved by 1% of the time
where the time goes in v5:
time: 153 us
  Pallas kernels  151 us (99%)
    pallas_call x1, Pallas kernels, device_fn(): pl.pallas_call(functools.partial(kernel, dims), out_shape=jax.ShapeDtypeS...  151 us

profile of v5, /device:TPU:97, one launch (start us, length us, event | category | flops | bytes accessed | tf_op | source)
XLA Modules:
  0.0 152.5 jit_solution(7043472683854306665)
XLA Ops:
  0.0 151.1 %shard_map.154 = f32[4,16,32]{2,1,0:T(8,128)} custom-call(bf16[2,1152]{1,0:T(2,128)(2,1)} %cond_ref.1, f32[2]{0:T(128)} %step_ref.1, bf16[16,1152]{1,0:T(8,128)(2,1)} %w_in_ref.1, bf16[2304]{0:T(1024)(128)(2,1)} %b_fa_ref.1, bf16[16,1152]{1,0:T(8,128)(2,1)} %bitcast.8, f32[4,16,32]{2,1,0:T(8,128)} %bitcast.9, bf16[4,32,1152]{2,1,0:T(8,128)(2,1)} %pos_hbm.1, ...), custom_call_target="tpu_custom_call" | custom-call | tf_op jit(solution)/shard_map/pallas_call | solution.py:476
  151.1 1.4 copy.18

commit v6 on v5

--- a/solution.py
+++ b/solution.py
@@ -386,10 +386,10 @@
         residual = hid_s[...].astype(jnp.float32) + mod(2) * proj
         mlp_in = (normalize(residual) * (1.0 + mod(3)) + mod(4)).astype(jnp.bfloat16)
         w_copy(2, layer).wait()
-        up_cols = up_w.shape[1] // 4
+        up_cols = up_w.shape[1] // 6
         w_copy(3, layer).wait()
         down = bias(14, 15)
-        for i in range(4):
+        for i in range(6):
             cols = slice(i * up_cols, (i + 1) * up_cols)
             up_bias = bias_s[pl.ds(layer, 1), 10 * width + i * up_cols:10 * width + (i + 1) * up_cols]
             up = jnp.dot(mlp_in, up_w[:, cols], preferred_element_type=jnp.float32) + up_bias

time: 153 us -> 156 us (1.020)
  Pallas kernels: 151 us -> 155 us
    pallas_call x1, Pallas kernels: 151 us -> 155 us  [device_fn(): pl.pallas_call(functools.partial(kernel, dims), out_shape=jax.ShapeDtypeS...]
where the time goes in v6:
time: 156 us
  Pallas kernels  155 us (99%)
    pallas_call x1, Pallas kernels, device_fn(): pl.pallas_call(functools.partial(kernel, dims), out_shape=jax.ShapeDtypeS...  155 us

profile of v6, /device:TPU:97, one launch (start us, length us, event | category | flops | bytes accessed | tf_op | source)
XLA Modules:
  0.0 156.0 jit_solution(15205895776839813214)
XLA Ops:
  0.0 154.6 %shard_map.154 = f32[4,16,32]{2,1,0:T(8,128)} custom-call(bf16[2,1152]{1,0:T(2,128)(2,1)} %cond_ref.1, f32[2]{0:T(128)} %step_ref.1, bf16[16,1152]{1,0:T(8,128)(2,1)} %w_in_ref.1, bf16[2304]{0:T(1024)(128)(2,1)} %b_fa_ref.1, bf16[16,1152]{1,0:T(8,128)(2,1)} %bitcast.8, f32[4,16,32]{2,1,0:T(8,128)} %bitcast.9, bf16[4,32,1152]{2,1,0:T(8,128)(2,1)} %pos_hbm.1, ...), custom_call_target="tpu_custom_call" | custom-call | tf_op jit(solution)/shard_map/pallas_call | solution.py:476
  154.7 1.4 copy.18
